TPU v7x, 256 devices: a whole 4x4x8 slice. The times are simulated.
256 devices in a mesh: dp: 8 (over z), vocab: 32 (over x, y, core).
Axes of the slice: x: 4, y: 4, z: 8, core: 2. Of those that a mesh axis runs over, the one named last changes fastest.
Arguments:
- token_ids: int32 [65536], P(('dp', 'vocab')), may hold values from 0 to 152063, as said below
- token_count: int32 [256], P(('dp', 'vocab')), may hold values from 16 to 256
- out_grads: bfloat16 [65536, 5120], P(('dp', 'vocab')), may hold values from -18 to 18
- master_rows: float32 [16384, 5120], P('vocab', 'dp'), may hold values from -0.8 to 0.8
- first_moment: float32 [16384, 5120], P('vocab', 'dp'), may hold values from -4 to 4
- second_moment: float32 [16384, 5120], P('vocab', 'dp'), may hold values from 0.001 to 1
Outputs:
- new_master: float32 [16384, 5120], P('vocab', 'dp')
- new_first: float32 [16384, 5120], P('vocab', 'dp')
- new_second: float32 [16384, 5120], P('vocab', 'dp')
- table_rows: bfloat16 [16384, 5120], P('vocab')
Inputs may be any that keep to these rules, and one draw needn't show every extreme that they name: `token_ids`: within each block of 256 slots, among the live slots (the first token_count of the block) at most 8 have ids in the new rows j * 512 + 135680 to (j + 1) * 512 + 135679 for any one j, and for some j exactly 8 in every block. Slots past token_count hold ids of new rows that are to be ignored.
All inputs are finite; a program needn't handle non-finite values.
Results may differ from a plain program's by a relative error of at most 0.001.
Values may be sent and summed in bfloat16 or wider, within the bound.
No kernel may reach another device: no remote copies, remote signals or barrier semaphores. Data moves between devices by JAX's collectives and lax.ppermute only.
A program may use at most 64 MiB of HBM per device.

v0:
```python
import jax
import jax.numpy as jnp
from jax import lax
from jax.sharding import PartitionSpec as P

VOCAB = 152064
CAP = 8


beta_one = 0.9
beta_two = 0.999
corr_one = 1.0 - 0.9**10
corr_two = 1.0 - 0.999**10
learn_rate = 0.01
epsilon = 1e-08


def body(token_ids, token_count, out_grads, master_rows, first_moment, second_moment):
    owners = lax.axis_size("vocab")
    groups = lax.axis_size("dp")
    rows_own = master_rows.shape[0]
    tok_slots = token_ids.shape[0]
    first_new = VOCAB - rows_own * owners
    position = jnp.arange(tok_slots)
    is_live = (position < token_count[0]) & (token_ids >= first_new)
    new_index = token_ids - first_new
    owner_of = new_index // rows_own
    row_in_owner = new_index % rows_own
    belongs = (owner_of[:, None] == jnp.arange(owners)[None, :]) & is_live[:, None]
    ranking = jnp.cumsum(belongs.astype(jnp.int32), axis=0) - 1
    my_rank = jnp.sum(jnp.where(belongs, ranking, 0), axis=1)
    slot_index = jnp.where(is_live, owner_of * CAP + my_rank, -1)
    placing = jnp.arange(owners * CAP)[:, None] == slot_index[None, :]
    outgoing = jnp.dot(
        placing.astype(jnp.bfloat16), out_grads, preferred_element_type=jnp.float32
    ).astype(jnp.bfloat16)
    slot_row = jnp.max(jnp.where(placing, row_in_owner[None, :], -1), axis=1)
    upper_part = jnp.where(slot_row >= 0, slot_row // 16, -1)
    lower_part = jnp.where(slot_row >= 0, slot_row % 16, 0)
    row_pairs = jnp.stack([upper_part, lower_part], axis=1).astype(jnp.bfloat16)
    tiled_pairs = jnp.tile(row_pairs, (1, groups))
    split_grads, split_pairs = (
        lax.all_to_all(outgoing, "dp", split_axis=1, concat_axis=0, tiled=True),
        lax.all_to_all(tiled_pairs, "dp", split_axis=1, concat_axis=0, tiled=True),
    )
    split_grads = split_grads.reshape(groups, owners * CAP, split_grads.shape[1])
    split_pairs = split_pairs.reshape(groups, owners * CAP, 2)
    arrived, arrived_pairs = (
        lax.all_to_all(split_grads, "vocab", split_axis=1, concat_axis=0, tiled=True),
        lax.all_to_all(split_pairs, "vocab", split_axis=1, concat_axis=0, tiled=True),
    )
    arrived = arrived.reshape(-1, arrived.shape[2])
    arrived_pairs = arrived_pairs.reshape(-1, 2).astype(jnp.float32)
    decoded = arrived_pairs[:, 0] * 16.0 + arrived_pairs[:, 1]
    selector = decoded[None, :] == jnp.arange(rows_own, dtype=jnp.float32)[:, None]
    gradient = jnp.dot(selector.astype(jnp.bfloat16), arrived, preferred_element_type=jnp.float32)
    new_first = beta_one * first_moment + (1.0 - beta_one) * gradient
    new_second = beta_two * second_moment + (1.0 - beta_two) * gradient * gradient
    update = new_first / corr_one / (jnp.sqrt(new_second / corr_two) + epsilon)
    new_master = master_rows - learn_rate * update
    table_rows = lax.all_gather(new_master.astype(jnp.bfloat16), "dp", axis=1, tiled=True)
    return (new_master, new_first, new_second, table_rows)


def solution(mesh):
    return jax.shard_map(
        body,
        mesh=mesh,
        in_specs=(
            P(("dp", "vocab")),
            P(("dp", "vocab")),
            P(("dp", "vocab"), None),
            P("vocab", "dp"),
            P("vocab", "dp"),
            P("vocab", "dp"),
        ),
        out_specs=(P("vocab", "dp"), P("vocab", "dp"), P("vocab", "dp"), P("vocab", None)),
        check_vma=False,
    )
```

profile of v0, /device:TPU:1, one launch (start us, length us, event | category | flops | bytes accessed | tf_op | source)
XLA Modules:
  0.0 226.1 jit_solution(13173120727746846813)
XLA Ops:
  8.0 0.7 and_select_fusion.2
  8.7 0.7 fusion.15
  9.4 0.7 compare_and_fusion
  10.0 0.6 reduce-window.6
  10.6 0.2 slice_reduce_fusion
  10.9 0.1 fusion.5
  11.0 0.7 add_select_fusion
  11.7 0.1 select_reduce_fusion
  11.8 0.6 tile.2
  12.4 9.0 %all-to-all-start = ((bf16[256,8,2]{0,2,1:T(2,128)(2,1)}), bf16[256,8,2]{0,2,1:T(2,128)(2,1)S(1)}, u32[]{:S(2)}, u32[]{:S(2)}) async-start(bf16[256,8,2]{0,2,1:T(2,128)(2,1)} %tile.2), calls=%async_computation | async-start | bytes 16384 | tf_op jit(solution)/shard_map/all_to_all | solution.py:44
  21.4 0.8 convolution_convert_fusion
  22.3 1.7 copy.51
  24.0 4.0 %all-to-all-done = bf16[256,8,2]{0,2,1:T(2,128)(2,1)S(1)} async-done(((bf16[256,8,2]{0,2,1:T(2,128)(2,1)}), bf16[256,8,2]{0,2,1:T(2,128)(2,1)S(1)}, u32[]{:S(2)}, u32[]{:S(2)}) %all-to-all-start) | async-done | bytes 8224 | tf_op jit(solution)/shard_map/all_to_all | solution.py:44
  28.0 4.4 %all-to-all-start.2 = ((bf16[256,8,640]{2,0,1:T(8,128)(2,1)}), bf16[256,8,640]{2,0,1:T(8,128)(2,1)}, u32[]{:S(2)}, u32[]{:S(2)}) async-start(bf16[256,8,640]{2,0,1:T(8,128)(2,1)} %bitcast.43), calls=%async_computation.2 | async-start | bytes 5242880 | tf_op jit(solution)/shard_map/all_to_all | solution.py:43
  32.4 0.8 copy.39
  33.2 58.8 %all-to-all-done.2 = bf16[256,8,640]{2,0,1:T(8,128)(2,1)} async-done(((bf16[256,8,640]{2,0,1:T(8,128)(2,1)}), bf16[256,8,640]{2,0,1:T(8,128)(2,1)}, u32[]{:S(2)}, u32[]{:S(2)}) %all-to-all-start.2) | async-done | bytes 2621472 | tf_op jit(solution)/shard_map/all_to_all | solution.py:43
  92.0 10.9 %all-to-all-start.1 = ((bf16[8,256,2]{0,2,1:T(2,128)(2,1)}), bf16[8,256,2]{0,2,1:T(2,128)(2,1)S(1)}, u32[]{:S(2)}, u32[]{:S(2)}) async-start(bf16[8,256,2]{0,2,1:T(2,128)(2,1)} %copy.39), calls=%async_computation.1 | async-start | bytes 262144 | tf_op jit(solution)/shard_map/all_to_all | solution.py:50
  103.0 4.7 %copy.43 = bf16[8,256,640]{2,0,1:T(8,128)(2,1)} copy(bf16[8,256,640]{2,1,0:T(8,128)(2,1)} %bitcast.8) | data formatting | bytes 5242880 | tf_op jit(solution)/shard_map/all_to_all | solution.py:43
  107.7 2.9 %all-to-all-done.1 = bf16[8,256,2]{0,2,1:T(2,128)(2,1)S(1)} async-done(((bf16[8,256,2]{0,2,1:T(2,128)(2,1)}), bf16[8,256,2]{0,2,1:T(2,128)(2,1)S(1)}, u32[]{:S(2)}, u32[]{:S(2)}) %all-to-all-start.1) | async-done | bytes 8224 | tf_op jit(solution)/shard_map/all_to_all | solution.py:50
  110.7 4.8 %all-to-all-start.3 = ((bf16[8,256,640]{2,0,1:T(8,128)(2,1)}), bf16[8,256,640]{2,0,1:T(8,128)(2,1)}, u32[]{:S(2)}, u32[]{:S(2)}) async-start(bf16[8,256,640]{2,0,1:T(8,128)(2,1)} %copy.43), calls=%async_computation.3 | async-start | bytes 5242880 | tf_op jit(solution)/shard_map/all_to_all | solution.py:49
  115.4 0.0 all-gather.2.cloned.1.call-start
  115.5 0.1 copy.40
  115.6 0.2 reshape.169
  115.8 0.2 copy.41
  115.9 0.2 reshape.168
  116.1 33.4 %all-to-all-done.3 = bf16[8,256,640]{2,0,1:T(8,128)(2,1)} async-done(((bf16[8,256,640]{2,0,1:T(8,128)(2,1)}), bf16[8,256,640]{2,0,1:T(8,128)(2,1)}, u32[]{:S(2)}, u32[]{:S(2)}) %all-to-all-start.3) | async-done | bytes 2621472 | tf_op jit(solution)/shard_map/all_to_all | solution.py:49
  149.5 2.4 %copy.45 = bf16[32,8,8,640]{3,2,1,0:T(8,128)(2,1)S(1)} copy(bf16[32,8,8,640]{3,1,2,0:T(8,128)(2,1)} %bitcast.11) | data formatting | bytes 5242880 | tf_op jit(solution)/shard_map/all_to_all | solution.py:49
  151.9 0.1 copy-done.2
  152.0 0.4 copy-done.3
  152.4 4.7 %fusion.11 = (bf16[512,640]{1,0:T(8,128)(2,1)}, f32[512,640]{1,0:T(8,128)}, f32[512,640]{1,0:T(8,128)}, f32[512,640]{1,0:T(8,128)}) fusion(f32[512,640]{1,0:T(8,128)S(1)} %copy-done.1, f32[512,640]{1,0:T(8,128)S(1)} %copy-done.2, f32[512,640]{1,0:T(8,128)S(1)} %copy-done.3, bf16[2048,640]{1,0:T(8,128)(2,1)S(1)} %bitcast.45, f32[2048]{0:T(1024)S(1)} %bitcast.49), kind=kOutput, calls=%fused_computation.43 | convolution fusion | flops 1347813376 | bytes 11149312 | tf_op jit(solution)/shard_map/dot_general | solution.py:56
  157.1 57.0 %all-gather.2.cloned.1.call-done = bf16[512,5120]{1,0:T(8,128)(2,1)} async-done(((bf16[512,640]{1,0:T(8,128)(2,1)}), bf16[512,5120]{1,0:T(8,128)(2,1)}) %all-gather.2.cloned.1.call-update) | async-done | bytes 5242896 | tf_op jit(solution)/shard_map/all_gather | solution.py:61
  214.1 5.2 %copy.54 = bf16[512,5120]{1,0:T(8,128)(2,1)} copy(bf16[512,5120]{1,0:T(8,128)(2,1)} %all-gather.2.cloned.1.call-done) | data formatting | bytes 10485760
  (13 shorter events, 0.1 us)
Async XLA Ops:
  7.2 14.3 %copy-start = (bf16[256,5120]{1,0:T(8,128)(2,1)S(1)}, bf16[256,5120]{1,0:T(8,128)(2,1)}, u32[]{:S(2)}) copy-start(bf16[256,5120]{1,0:T(8,128)(2,1)} %param.8) | copy-start | bytes 7864324
  12.4 15.6 %all-to-all-start = ((bf16[256,8,2]{0,2,1:T(2,128)(2,1)}), bf16[256,8,2]{0,2,1:T(2,128)(2,1)S(1)}, u32[]{:S(2)}, u32[]{:S(2)}) async-start(bf16[256,8,2]{0,2,1:T(2,128)(2,1)} %tile.2), calls=%async_computation | async-start | bytes 16384 | tf_op jit(solution)/shard_map/all_to_all | solution.py:44
  28.0 64.0 %all-to-all-start.2 = ((bf16[256,8,640]{2,0,1:T(8,128)(2,1)}), bf16[256,8,640]{2,0,1:T(8,128)(2,1)}, u32[]{:S(2)}, u32[]{:S(2)}) async-start(bf16[256,8,640]{2,0,1:T(8,128)(2,1)} %bitcast.43), calls=%async_computation.2 | async-start | bytes 5242880 | tf_op jit(solution)/shard_map/all_to_all | solution.py:43
  92.0 18.6 %all-to-all-start.1 = ((bf16[8,256,2]{0,2,1:T(2,128)(2,1)}), bf16[8,256,2]{0,2,1:T(2,128)(2,1)S(1)}, u32[]{:S(2)}, u32[]{:S(2)}) async-start(bf16[8,256,2]{0,2,1:T(2,128)(2,1)} %copy.39), calls=%async_computation.1 | async-start | bytes 262144 | tf_op jit(solution)/shard_map/all_to_all | solution.py:50
  110.7 38.9 %all-to-all-start.3 = ((bf16[8,256,640]{2,0,1:T(8,128)(2,1)}), bf16[8,256,640]{2,0,1:T(8,128)(2,1)}, u32[]{:S(2)}, u32[]{:S(2)}) async-start(bf16[8,256,640]{2,0,1:T(8,128)(2,1)} %copy.43), calls=%async_computation.3 | async-start | bytes 5242880 | tf_op jit(solution)/shard_map/all_to_all | solution.py:49
  115.4 98.7 %all-gather.2.cloned.1.call-start = ((), (), s32[]{:S(2)}) async-start(), calls=%async_computation.4 | async-start | bytes 5898240 | tf_op jit(solution)/shard_map/all_gather | solution.py:61
  149.5 2.4 %copy-start.1 = (f32[512,640]{1,0:T(8,128)S(1)}, f32[512,640]{1,0:T(8,128)}, u32[]{:S(2)}) copy-start(f32[512,640]{1,0:T(8,128)} %param.9) | copy-start | bytes 3932164
  149.5 2.5 %copy-start.2 = (f32[512,640]{1,0:T(8,128)S(1)}, f32[512,640]{1,0:T(8,128)}, u32[]{:S(2)}) copy-start(f32[512,640]{1,0:T(8,128)} %param.10) | copy-start | bytes 3932164
  149.5 2.9 %copy-start.3 = (f32[512,640]{1,0:T(8,128)S(1)}, f32[512,640]{1,0:T(8,128)}, u32[]{:S(2)}) copy-start(f32[512,640]{1,0:T(8,128)} %param.11) | copy-start | bytes 3932164
Sparse Core Ops, SparseCore 0:
  157.2 56.8 all-gather.1
where the time goes:
time: 227 us; the launch traced here: 226 us
  waiting for transfers between devices  156 us (69%)
  starting transfers between devices  29.2 us (13%)
  local copies, waits for them, and re-layouts  16.7 us (7%)
  between operations  14.9 us (7%)
  matrix products  5.52 us (2%)
  other arithmetic  3.65 us (2%)
    all_to_all x1, waiting for transfers between devices, body(): lax.all_to_all(outgoing, 'dp', split_axis=1, concat_axis=0, tiled=True)  58.8 us
    all_gather x1, waiting for transfers between devices, body(): lax.all_gather(new_master.astype(jnp.bfloat16), 'dp', axis=1, tiled=True)  57 us
    all_to_all x1, waiting for transfers between devices, body(): lax.all_to_all(split_grads, 'vocab', split_axis=1, concat_axis=0, tiled=T...  33.4 us
    all_to_all x1, starting transfers between devices, body(): lax.all_to_all(split_pairs, 'vocab', split_axis=1, concat_axis=0, tiled=T...  10.9 us
    all_to_all x1, starting transfers between devices, body(): lax.all_to_all(tiled_pairs, 'dp', split_axis=1, concat_axis=0, tiled=True)  9 us
    all_to_all x2, local copies, waits for them, and re-layouts, body(): lax.all_to_all(outgoing, 'dp', split_axis=1, concat_axis=0, tiled=True)  6.47 us
    unnamed x9, local copies, waits for them, and re-layouts  5.69 us
    all_to_all x1, starting transfers between devices, body(): lax.all_to_all(split_grads, 'vocab', split_axis=1, concat_axis=0, tiled=T...  4.79 us
  transfers between devices with their start and end apart: 5, of which 5 were waited for; matrix products, arithmetic and copies ran while one was open for 4% of the time, Pallas kernels for 0%

commit v1 on v0

v1 whole, which is shorter than its diff:
```python
import functools

import jax
import jax.numpy as jnp
from jax import lax
from jax.experimental import pallas as pl
from jax.experimental.pallas import tpu as pltpu
from jax.sharding import PartitionSpec as P


VOCAB = 152064
CAP = 8

beta_one = 0.9
beta_two = 0.999
corr_one = 1.0 - 0.9**10
corr_two = 1.0 - 0.999**10
learn_rate = 0.01
epsilon = 1e-08


def near(x):
    return pltpu.with_memory_space_constraint(x, pltpu.VMEM)


def far(x):
    return pltpu.with_memory_space_constraint(x, pltpu.HBM)


SM = pl.BlockSpec(memory_space=pltpu.SMEM)
VM = pl.BlockSpec(memory_space=pltpu.VMEM)
HB = pl.BlockSpec(memory_space=pltpu.HBM)


def kernel(fn, out_shape, in_specs, out_specs, vmem_limit=24 << 20, **kw):
    def call(*args):
        return pl.pallas_call(
            fn,
            out_shape=out_shape,
            in_specs=in_specs,
            out_specs=out_specs,
            compiler_params=pltpu.CompilerParams(vmem_limit_bytes=vmem_limit),
            **kw,
        )(*args)

    return call


def prep_kernel(count_ref, ids_ref, grads_ref, out_ref, local_ref, buf, sems, *, owners, groups, rows_own, cols):
    slots = ids_ref.shape[1]
    copies = [pltpu.make_async_copy(grads_ref.at[:, g * cols : (g + 1) * cols], buf.at[g], sems.at[g]) for g in range(groups)]
    for c in copies:
        c.start()
    first_new = VOCAB - rows_own * owners
    ids = ids_ref[...]
    position = lax.broadcasted_iota(jnp.int32, (1, slots), 1)
    live = (position < count_ref[0]) & (ids >= first_new)
    local = jnp.where(live, ids - first_new, -1)
    local_ref[...] = local
    owner = jnp.where(live, local // rows_own, -1)
    key_row = jnp.broadcast_to(owner, (slots, slots))
    key_col = key_row.T
    lane = lax.broadcasted_iota(jnp.int32, (slots, slots), 1)
    sub = lax.broadcasted_iota(jnp.int32, (slots, slots), 0)
    earlier = (key_row == key_col) & (sub < lane)
    rank = jnp.sum(earlier.astype(jnp.int32), axis=0, keepdims=True)
    place = jnp.where(live, owner * CAP + rank, -1)
    placing = (sub == jnp.broadcast_to(place, (slots, slots))).astype(jnp.bfloat16)
    for g in range(groups):
        copies[g].wait()
        got = jnp.dot(placing, buf[g], preferred_element_type=jnp.float32).astype(jnp.bfloat16)
        out_ref[g * owners : (g + 1) * owners] = got.reshape(owners, CAP, cols)


def rows_kernel(mine_ref, local_ref, out_ref, *, rows_own):
    owners, slots = local_ref.shape
    mine = mine_ref[0]
    local = local_ref[...]
    here = (local >= mine * rows_own) & (local < (mine + 1) * rows_own)
    row = jnp.where(here, local - mine * rows_own, 0)
    sub = lax.broadcasted_iota(jnp.int32, (slots, slots), 0)
    lane = lax.broadcasted_iota(jnp.int32, (slots, slots), 1)
    ahead = (sub < lane).astype(jnp.bfloat16)
    rank = jnp.dot(here.astype(jnp.bfloat16), ahead, preferred_element_type=jnp.float32)
    lanes = lax.broadcasted_iota(jnp.int32, (owners, slots), 1)
    total = jnp.zeros((owners, slots), jnp.int32)
    for s in range(CAP):
        picked = jnp.where(here & (rank == float(s)), row + 1, 0)
        total = jnp.where(lax.rem(lanes, CAP) == s, jnp.sum(picked, axis=1, keepdims=True), total)
    source = lax.broadcasted_iota(jnp.int32, (owners, slots), 0) ^ mine
    codes = jnp.sum(jnp.where(lanes // CAP == source, total, 0), axis=0, keepdims=True) - 1
    out_ref[...] = jnp.broadcast_to(codes, out_ref.shape)


def adam(gradient, first, second, master):
    new_first = beta_one * first + (1.0 - beta_one) * gradient
    new_second = beta_two * second + (1.0 - beta_two) * gradient * gradient
    update = new_first / corr_one / (jnp.sqrt(new_second / corr_two) + epsilon)
    return new_first, new_second, master - learn_rate * update


def adam_kernel(where_ref, tokens_ref, *refs, owners, groups, at, width, pieces, aliased):
    codes, refs = refs[:groups], refs[groups:]
    state, refs = refs[:3], refs[3 + (3 if aliased else 0) :]
    outs, refs = refs[:3], refs[3:]
    piece_refs, refs = refs[: len(pieces)], refs[len(pieces) :]
    code_buf, b0, b1, b2, sems = refs
    bufs = (b0, b1, b2)
    into = [pltpu.make_async_copy(r.at[:, pl.ds(at, width)], b, sems.at[i]) for i, (r, b) in enumerate(zip(state, bufs))]
    for c in into:
        c.start()
    rows_own = b0.shape[0]
    slots = owners * CAP
    z = where_ref[0]
    for k in range(groups):
        code_buf[lax.rem(z + groups - k, groups)] = codes[k][...]
    sub = lax.broadcasted_iota(jnp.int32, (rows_own, slots), 0)
    gradient = None
    for g in range(groups):
        code = jnp.broadcast_to(code_buf[g, 0:1, :], (rows_own, slots))
        selector = (sub == code).astype(jnp.bfloat16)
        data = tokens_ref[g * owners : (g + 1) * owners, :, at : at + width].reshape(slots, width)
        part = jnp.dot(selector, data, preferred_element_type=jnp.float32)
        gradient = part if gradient is None else gradient + part
    for c in into:
        c.wait()
    new_first, new_second, new_master = adam(gradient, b1[...], b2[...], b0[...])
    rounded = new_master.astype(jnp.bfloat16)
    b0[...] = new_master
    b1[...] = new_first
    b2[...] = new_second
    out = [pltpu.make_async_copy(b, r.at[:, pl.ds(at, width)], sems.at[i]) for i, (r, b) in enumerate(zip(outs, bufs))]
    for c in out:
        c.start()
    done = 0
    for piece_ref, w in zip(piece_refs, pieces):
        piece_ref[...] = rounded[:, done : done + w]
        done += w
    for c in out:
        c.wait()


def put_kernel(where_ref, *refs, spots, cols, groups, aliased):
    count = len(spots)
    ins = refs[:count]
    table_ref = refs[count + (1 if aliased else 0)]
    sem = refs[-1]
    z = where_ref[0]
    copies = []
    for i, (shift, row, off) in enumerate(spots):
        n, w = ins[i].shape
        g = lax.rem(z + groups - shift, groups)
        at = pl.multiple_of(g * cols + off, 128)
        copies.append(pltpu.make_async_copy(ins[i], table_ref.at[pl.ds(row, n), pl.ds(at, w)], sem.at[i]))
    for c in copies:
        c.start()
    for c in copies:
        c.wait()


def put(table, where, pieces, shape, cols, groups):
    arrays = [near(p[0]) for p in pieces]
    spots = tuple(p[1:] for p in pieces)
    aliased = table is not None
    extra = [far(table)] if aliased else []
    return kernel(
        functools.partial(put_kernel, spots=spots, cols=cols, groups=groups, aliased=aliased),
        jax.ShapeDtypeStruct(shape, jnp.bfloat16),
        [SM] + [VM for _ in arrays] + [HB for _ in extra],
        HB,
        input_output_aliases={len(arrays) + 1: 0} if aliased else {},
        scratch_shapes=[pltpu.SemaphoreType.DMA((len(arrays),))],
    )(where, *arrays, *extra)


def shift_by(x, k, groups):
    return lax.ppermute(x, "dp", [(i, (i + k) % groups) for i in range(groups)])


def ring(piece, off, groups):
    half = groups // 2
    rows = piece.shape[0]
    got = [(piece, 0, 0, off)]
    up = down = piece
    for s in range(1, half):
        up = shift_by(up, 1, groups)
        down = shift_by(down, -1, groups)
        got += [(up, s, 0, off), (down, groups - s, 0, off)]
    last = [
        (shift_by(up[: rows // 2], 1, groups), half, 0, off),
        (shift_by(down[rows // 2 :], -1, groups), half, rows // 2, off),
    ]
    return got, last


def step(token_ids, token_count, out_grads, master_rows, first_moment, second_moment):
    owners = lax.axis_size("vocab")
    groups = lax.axis_size("dp")
    rows_own, cols = master_rows.shape
    slots = token_ids.shape[0]
    bf16, i32 = jnp.bfloat16, jnp.int32
    z = lax.axis_index("dp").astype(i32).reshape(1)
    mine = lax.axis_index("vocab").astype(i32).reshape(1)
    sizes = dict(owners=owners, groups=groups)
    state = jax.ShapeDtypeStruct((rows_own, cols), jnp.float32)
    master_rows, first_moment, second_moment = far(master_rows), far(first_moment), far(second_moment)

    outgoing, local = kernel(
        functools.partial(prep_kernel, rows_own=rows_own, cols=cols, **sizes),
        [pltpu.VMEM((groups * owners, CAP, cols), bf16), pltpu.VMEM((1, slots), i32)],
        [SM, VM, HB],
        [VM, VM],
        scratch_shapes=[pltpu.VMEM((groups, slots, cols), bf16), pltpu.SemaphoreType.DMA((groups,))],
    )(token_count, token_ids.reshape(1, slots), far(out_grads))
    tokens = lax.all_to_all(outgoing, ("dp", "vocab"), split_axis=0, concat_axis=0, tiled=True)
    reach = 1
    while reach < owners:
        other = lax.ppermute(local, "vocab", [(i, i ^ reach) for i in range(owners)])
        local = jnp.concatenate([local, other], 0)
        reach *= 2
    codes = kernel(
        functools.partial(rows_kernel, rows_own=rows_own),
        jax.ShapeDtypeStruct((8, slots), i32),
        [SM, pl.BlockSpec()],
        pl.BlockSpec(),
    )(mine, local)
    codes = [codes] + [shift_by(codes, k, groups) for k in range(1, groups)]

    def adam_part(at, pieces, previous):
        width = sum(pieces)
        aliased = previous is not None
        n_in = 2 + groups + 3
        return kernel(
            functools.partial(adam_kernel, at=at, width=width, pieces=pieces, aliased=aliased, **sizes),
            [state] * 3 + [pltpu.VMEM((rows_own, w), bf16) for w in pieces],
            [SM, VM] + [pl.BlockSpec()] * groups + [HB] * (6 if aliased else 3),
            [HB] * 3 + [VM] * len(pieces),
            input_output_aliases={n_in + i: i for i in range(3)} if aliased else {},
            scratch_shapes=[pltpu.VMEM((groups, 8, slots), i32)]
            + [pltpu.VMEM((rows_own, width), jnp.float32)] * 3
            + [pltpu.SemaphoreType.DMA((3,))],
        )(z, near(tokens), *codes, master_rows, first_moment, second_moment, *(map(far, previous) if aliased else ()))

    *new_state, piece_a = adam_part(0, (256,), None)
    *new_state, piece_b, piece_c = adam_part(256, (256, cols - 512), new_state)
    shape = (rows_own, cols * groups)
    got_a, last_a = ring(piece_a, 0, groups)
    got_b, last_b = ring(piece_b, 256, groups)
    got_c, last_c = ring(piece_c, 512, groups)
    half = len(got_a) - 2
    table = put(None, z, got_a[:half] + got_b[:half] + got_c[:half], shape, cols, groups)
    table = put(table, z, got_a[half:] + got_b[half:] + got_c[half:], shape, cols, groups)
    table = put(table, z, last_a + last_b + last_c, shape, cols, groups)
    return (*new_state, table)


def solution(mesh):
    return jax.shard_map(
        step,
        mesh=mesh,
        in_specs=(
            P(("dp", "vocab")),
            P(("dp", "vocab")),
            P(("dp", "vocab"), None),
            P("vocab", "dp"),
            P("vocab", "dp"),
            P("vocab", "dp"),
        ),
        out_specs=(P("vocab", "dp"), P("vocab", "dp"), P("vocab", "dp"), P("vocab", None)),
        check_vma=False,
    )
```

time: 227 us -> 161 us (0.71)
  the two profiles are of different devices: /device:TPU:1 before, /device:TPU:26 now
where the time goes in v1:
time: 161 us
  waiting for transfers between devices  72.2 us (45%)
  starting transfers between devices  69.7 us (43%)
  Pallas kernels  15.4 us (10%)
  local copies, waits for them, and re-layouts  2.25 us (1%)
  between operations  1.67 us (1%)
    ppermute x31, waiting for transfers between devices, shift_by(): return lax.ppermute(x, 'dp', [(i, (i + k) % groups) for i in range(groups)])  58.5 us
    ppermute x31, starting transfers between devices, shift_by(): return lax.ppermute(x, 'dp', [(i, (i + k) % groups) for i in range(groups)])  49.3 us
    pallas_call x7, Pallas kernels, call(): pl.pallas_call(fn, out_shape=out_shape, in_specs=in_specs, out_specs=out_...  15.4 us
    all_to_all x1, starting transfers between devices, step(): lax.all_to_all(outgoing, ('dp', 'vocab'), split_axis=0, concat_axis=0, ti...  14.4 us
    ppermute x5, waiting for transfers between devices, step(): lax.ppermute(local, 'vocab', [(i, i ^ reach) for i in range(owners)])  13.7 us
    ppermute x5, starting transfers between devices, step(): lax.ppermute(local, 'vocab', [(i, i ^ reach) for i in range(owners)])  5.91 us
  transfers between devices with their start and end apart: 37, of which 12 were waited for; matrix products, arithmetic and copies ran while one was open for 0% of the time, Pallas kernels for 2%

profile of v1, /device:TPU:26, one launch (start us, length us, event | category | flops | bytes accessed | tf_op | source)
XLA Modules:
  0.0 161.2 jit_solution(13161095609260965251)
XLA Ops:
  2.0 3.5 %shard_map.93 = (bf16[256,8,640]{2,1,0:T(8,128)(2,1)S(1)}, s32[1,256]{1,0:T(1,128)S(1)}) custom-call(s32[1]{0:T(128)S(6)} %copy.20.count_ref, s32[1,256]{1,0:T(1,128)S(1)} %bitcast.3, bf16[256,5120]{1,0:T(8,128)(2,1)} %grads_ref.1), custom_call_target="tpu_custom_call" | custom-call | tf_op jit(solution)/shard_map/pallas_call | solution.py:37
  5.4 1.5 copy-done
  6.9 14.4 %all-to-all-start = ((bf16[256,8,640]{2,1,0:T(8,128)(2,1)}), bf16[256,8,640]{2,1,0:T(8,128)(2,1)S(1)}, u32[]{:S(2)}, u32[]{:S(2)}) async-start(bf16[256,8,640]{2,1,0:T(8,128)(2,1)} %copy-done), calls=%async_computation | async-start | bytes 5242880 | tf_op jit(solution)/shard_map/all_to_all | solution.py:215
  23.4 3.2 %collective-permute-done.1 = s32[2,256]{1,0:T(2,128)S(1)} collective-permute-done((s32[2,256]{1,0:T(2,128)S(1)}, s32[2,256]{1,0:T(2,128)S(1)}, u32[]{:S(2)}, u32[]{:S(2)}) %collective-permute-start.1) | collective-permute-done | bytes 2080 | tf_op jit(solution)/shard_map/ppermute | solution.py:218
  26.6 1.5 collective-permute-start.2
  28.1 3.7 %collective-permute-done.2 = s32[4,256]{1,0:T(4,128)S(1)} collective-permute-done((s32[4,256]{1,0:T(4,128)S(1)}, s32[4,256]{1,0:T(4,128)S(1)}, u32[]{:S(2)}, u32[]{:S(2)}) %collective-permute-start.2) | collective-permute-done | bytes 4128 | tf_op jit(solution)/shard_map/ppermute | solution.py:218
  33.2 2.4 %collective-permute-done.3 = s32[8,256]{1,0:T(8,128)S(1)} collective-permute-done((s32[8,256]{1,0:T(8,128)S(1)}, s32[8,256]{1,0:T(8,128)S(1)}, u32[]{:S(2)}, u32[]{:S(2)}) %collective-permute-start.3) | collective-permute-done | bytes 8224 | tf_op jit(solution)/shard_map/ppermute | solution.py:218
  35.6 2.0 %collective-permute-start.4 = (s32[16,256]{1,0:T(8,128)S(1)}, s32[16,256]{1,0:T(8,128)S(1)}, u32[]{:S(2)}, u32[]{:S(2)}) collective-permute-start(s32[16,256]{1,0:T(8,128)S(1)} %concatenate.22), channel_id=1, source_target_pairs={{0,16},{1,17},{2,18},{3,19},{4,20},{5,21},{6,22},{7,23},{8,24},{9,... | collective-permute-start | bytes 49160 | tf_op jit(solution)/shard_map/ppermute | solution.py:218
  37.6 3.4 %collective-permute-done.4 = s32[16,256]{1,0:T(8,128)S(1)} collective-permute-done((s32[16,256]{1,0:T(8,128)S(1)}, s32[16,256]{1,0:T(8,128)S(1)}, u32[]{:S(2)}, u32[]{:S(2)}) %collective-permute-start.4) | collective-permute-done | bytes 16416 | tf_op jit(solution)/shard_map/ppermute | solution.py:218
  41.3 5.1 %collective-permute-start.10 = (s32[8,256]{1,0:T(8,128)S(1)}, s32[8,256]{1,0:T(8,128)S(1)}, u32[]{:S(2)}, u32[]{:S(2)}) collective-permute-start(s32[8,256]{1,0:T(8,128)S(1)} %shard_map.94.refs_0_), channel_id=1, source_target_pairs={{0,192},{32,224},{64,0},{96,32},{128,64},{160,96},{192,128},{224,1... | collective-permute-start | bytes 24584 | tf_op jit(solution)/shard_map/ppermute | solution.py:177
  48.9 4.1 %collective-permute-start.7 = (s32[8,256]{1,0:T(8,128)S(1)}, s32[8,256]{1,0:T(8,128)S(1)}, u32[]{:S(2)}, u32[]{:S(2)}) collective-permute-start(s32[8,256]{1,0:T(8,128)S(1)} %shard_map.94.refs_0_), channel_id=1, source_target_pairs={{0,96},{32,128},{64,160},{96,192},{128,224},{160,0},{192,32},{224,... | collective-permute-start | bytes 24584 | tf_op jit(solution)/shard_map/ppermute | solution.py:177
  53.0 25.8 %collective-permute-done.10.refs_6_ = s32[8,256]{1,0:T(8,128)S(1)} collective-permute-done((s32[8,256]{1,0:T(8,128)S(1)}, s32[8,256]{1,0:T(8,128)S(1)}, u32[]{:S(2)}, u32[]{:S(2)}) %collective-permute-start.10) | collective-permute-done | bytes 8224 | tf_op jit(solution)/shard_map/ppermute | solution.py:177
  78.8 5.4 %collective-permute-start.8 = (s32[8,256]{1,0:T(8,128)S(1)}, s32[8,256]{1,0:T(8,128)S(1)}, u32[]{:S(2)}, u32[]{:S(2)}) collective-permute-start(s32[8,256]{1,0:T(8,128)S(1)} %shard_map.94.refs_0_), channel_id=1, source_target_pairs={{0,128},{32,160},{64,192},{96,224},{128,0},{160,32},{192,64},{224,... | collective-permute-start | bytes 24584 | tf_op jit(solution)/shard_map/ppermute | solution.py:177
  84.2 2.2 %collective-permute-done.8.refs_4_ = s32[8,256]{1,0:T(8,128)S(1)} collective-permute-done((s32[8,256]{1,0:T(8,128)S(1)}, s32[8,256]{1,0:T(8,128)S(1)}, u32[]{:S(2)}, u32[]{:S(2)}) %collective-permute-start.8) | collective-permute-done | bytes 8224 | tf_op jit(solution)/shard_map/ppermute | solution.py:177
  86.5 3.2 %collective-permute-done.9.refs_5_ = s32[8,256]{1,0:T(8,128)S(1)} collective-permute-done((s32[8,256]{1,0:T(8,128)S(1)}, s32[8,256]{1,0:T(8,128)S(1)}, u32[]{:S(2)}, u32[]{:S(2)}) %collective-permute-start.9) | collective-permute-done | bytes 8224 | tf_op jit(solution)/shard_map/ppermute | solution.py:177
  89.7 3.3 %shard_map.95 = (f32[512,640]{1,0:T(8,128)}, f32[512,640]{1,0:T(8,128)}, f32[512,640]{1,0:T(8,128)}, bf16[512,256]{1,0:T(8,128)(2,1)S(1)}) custom-call(s32[1]{0:T(128)} %bitcast.where_ref, bf16[256,8,640]{2,1,0:T(8,128)(2,1)S(1)} %all-to-all-done.tokens_ref, s32[8,256]{1,0:T(8,128)S(1)} %shard_map.94.refs_0_, s32[8,256]{1,0:T(8,128)S(1)} %collective-permute-done.5.refs_1_, ...), custom_call_target="tpu_custom_call" | custom-call | tf_op jit(solution)/shard_map/pallas_call | solution.py:37
  92.9 4.5 %shard_map.96 = (f32[512,640]{1,0:T(8,128)}, f32[512,640]{1,0:T(8,128)}, f32[512,640]{1,0:T(8,128)}, bf16[512,256]{1,0:T(8,128)(2,1)S(1)}, bf16[512,128]{1,0:T(8,128)(2,1)S(1)}) custom-call(s32[1]{0:T(128)} %bitcast.where_ref, bf16[256,8,640]{2,1,0:T(8,128)(2,1)S(1)} %all-to-all-done.tokens_ref, ...), custom_call_target="tpu_custom_call", output_to_operand_aliasing={{0}: (13, {}), {1}: (14, {}), {2}: (15, {})} | custom-call | tf_op jit(solution)/shard_map/pallas_call | solution.py:37
  98.8 3.1 %collective-permute-start.24 = (bf16[512,256]{1,0:T(8,128)(2,1)S(1)}, bf16[512,256]{1,0:T(8,128)(2,1)S(1)}, u32[]{:S(2)}, u32[]{:S(2)}) collective-permute-start(bf16[512,256]{1,0:T(8,128)(2,1)S(1)} %get-tuple-element.24.refs_5_), channel_id=1, source_target_pairs={{0,224},{32,0},{64,32},{96,64},{128,96},{160,128},{192,160},{224,1... | collective-permute-start | bytes 786440 | tf_op jit(solution)/shard_map/ppermute | solution.py:177
  101.9 3.2 %collective-permute-start.16 = (bf16[512,256]{1,0:T(8,128)(2,1)S(1)}, bf16[512,256]{1,0:T(8,128)(2,1)S(1)}, u32[]{:S(2)}, u32[]{:S(2)}) collective-permute-start(bf16[512,256]{1,0:T(8,128)(2,1)S(1)} %get-tuple-element.23.refs_0_), channel_id=1, source_target_pairs={{0,224},{32,0},{64,32},{96,64},{128,96},{160,128},{192,160},{224,1... | collective-permute-start | bytes 786440 | tf_op jit(solution)/shard_map/ppermute | solution.py:177
  105.1 9.4 %collective-permute-done.28.refs_11_ = bf16[512,128]{1,0:T(8,128)(2,1)S(1)} collective-permute-done((bf16[512,128]{1,0:T(8,128)(2,1)S(1)}, bf16[512,128]{1,0:T(8,128)(2,1)S(1)}, u32[]{:S(2)}, u32[]{:S(2)}) %collective-permute-start.28) | collective-permute-done | bytes 131104 | tf_op jit(solution)/shard_map/ppermute | solution.py:177
  114.5 2.2 %collective-permute-start.32 = (bf16[512,128]{1,0:T(8,128)(2,1)S(1)}, bf16[512,128]{1,0:T(8,128)(2,1)S(1)}, u32[]{:S(2)}, u32[]{:S(2)}) collective-permute-start(bf16[512,128]{1,0:T(8,128)(2,1)S(1)} %get-tuple-element.25.refs_10_), channel_id=1, source_target_pairs={{0,224},{32,0},{64,32},{96,64},{128,96},{160,128},{192,160},{224,1... | collective-permute-start | bytes 393224 | tf_op jit(solution)/shard_map/ppermute | solution.py:177
  116.7 3.2 %collective-permute-start.25 = (bf16[512,256]{1,0:T(8,128)(2,1)S(1)}, bf16[512,256]{1,0:T(8,128)(2,1)S(1)}, u32[]{:S(2)}, u32[]{:S(2)}) collective-permute-start(bf16[512,256]{1,0:T(8,128)(2,1)S(1)} %collective-permute-done.24.refs_7_), channel_id=1, source_target_pairs={{0,224},{32,0},{64,32},{96,64},{128,96},{160,128},{192,160},{224,1... | collective-permute-start | bytes 786440 | tf_op jit(solution)/shard_map/ppermute | solution.py:177
  119.9 3.2 %collective-permute-start.17 = (bf16[512,256]{1,0:T(8,128)(2,1)S(1)}, bf16[512,256]{1,0:T(8,128)(2,1)S(1)}, u32[]{:S(2)}, u32[]{:S(2)}) collective-permute-start(bf16[512,256]{1,0:T(8,128)(2,1)S(1)} %collective-permute-done.16.refs_2_), channel_id=1, source_target_pairs={{0,224},{32,0},{64,32},{96,64},{128,96},{160,128},{192,160},{224,1... | collective-permute-start | bytes 786440 | tf_op jit(solution)/shard_map/ppermute | solution.py:177
  123.2 8.4 %collective-permute-done.29.refs_13_ = bf16[512,128]{1,0:T(8,128)(2,1)S(1)} collective-permute-done((bf16[512,128]{1,0:T(8,128)(2,1)S(1)}, bf16[512,128]{1,0:T(8,128)(2,1)S(1)}, u32[]{:S(2)}, u32[]{:S(2)}) %collective-permute-start.29) | collective-permute-done | bytes 131104 | tf_op jit(solution)/shard_map/ppermute | solution.py:177
  132.1 1.5 collective-permute-start.22
  133.6 1.7 %collective-permute-start.26 = (bf16[512,256]{1,0:T(8,128)(2,1)S(1)}, bf16[512,256]{1,0:T(8,128)(2,1)S(1)}, u32[]{:S(2)}, u32[]{:S(2)}) collective-permute-start(bf16[512,256]{1,0:T(8,128)(2,1)S(1)} %collective-permute-done.25.refs_9_), channel_id=1, source_target_pairs={{0,224},{32,0},{64,32},{96,64},{128,96},{160,128},{192,160},{224,1... | collective-permute-start | bytes 786440 | tf_op jit(solution)/shard_map/ppermute | solution.py:177
  135.6 3.0 %collective-permute-start.18 = (bf16[512,256]{1,0:T(8,128)(2,1)S(1)}, bf16[512,256]{1,0:T(8,128)(2,1)S(1)}, u32[]{:S(2)}, u32[]{:S(2)}) collective-permute-start(bf16[512,256]{1,0:T(8,128)(2,1)S(1)} %collective-permute-done.17.refs_4_), channel_id=1, source_target_pairs={{0,224},{32,0},{64,32},{96,64},{128,96},{160,128},{192,160},{224,1... | collective-permute-start | bytes 786440 | tf_op jit(solution)/shard_map/ppermute | solution.py:177
  138.6 8.2 %collective-permute-done.30.refs_4_ = bf16[512,128]{1,0:T(8,128)(2,1)S(1)} collective-permute-done((bf16[512,128]{1,0:T(8,128)(2,1)S(1)}, bf16[512,128]{1,0:T(8,128)(2,1)S(1)}, u32[]{:S(2)}, u32[]{:S(2)}) %collective-permute-start.30) | collective-permute-done | bytes 131104 | tf_op jit(solution)/shard_map/ppermute | solution.py:177
  146.8 2.1 %collective-permute-start.31 = (bf16[256,128]{1,0:T(8,128)(2,1)S(1)}, bf16[256,128]{1,0:T(8,128)(2,1)S(1)}, u32[]{:S(2)}, u32[]{:S(2)}) collective-permute-start(bf16[256,128]{1,0:T(8,128)(2,1)S(1)} %slice.28), channel_id=1, source_target_pairs={{0,32},{32,64},{64,96},{96,128},{128,160},{160,192},{192,224},{224... | collective-permute-start | bytes 196616 | tf_op jit(solution)/shard_map/ppermute | solution.py:177
  149.0 3.3 %collective-permute-start.27 = (bf16[256,256]{1,0:T(8,128)(2,1)S(1)}, bf16[256,256]{1,0:T(8,128)(2,1)S(1)}, u32[]{:S(2)}, u32[]{:S(2)}) collective-permute-start(bf16[256,256]{1,0:T(8,128)(2,1)S(1)} %slice.27), channel_id=1, source_target_pairs={{0,224},{32,0},{64,32},{96,64},{128,96},{160,128},{192,160},{224,1... | collective-permute-start | bytes 393224 | tf_op jit(solution)/shard_map/ppermute | solution.py:177
  152.4 3.3 %collective-permute-start.19 = (bf16[256,256]{1,0:T(8,128)(2,1)S(1)}, bf16[256,256]{1,0:T(8,128)(2,1)S(1)}, u32[]{:S(2)}, u32[]{:S(2)}) collective-permute-start(bf16[256,256]{1,0:T(8,128)(2,1)S(1)} %slice.25), channel_id=1, source_target_pairs={{0,224},{32,0},{64,32},{96,64},{128,96},{160,128},{192,160},{224,1... | collective-permute-start | bytes 393224 | tf_op jit(solution)/shard_map/ppermute | solution.py:177
  155.8 1.8 %shard_map.97.refs_6_ = bf16[512,5120]{1,0:T(8,128)(2,1)} custom-call(s32[1]{0:T(128)} %bitcast.where_ref, bf16[512,256]{1,0:T(8,128)(2,1)S(1)} %get-tuple-element.23.refs_0_, bf16[512,256]{1,0:T(8,128)(2,1)S(1)} %collective-permute-done.12.refs_1_, bf16[512,256]{1,0:T(8,128)(2,1)S(1)} %collective-permute-done.16.refs_2_, ...), custom_call_target="tpu_custom_call" | custom-call | tf_op jit(solution)/shard_map/pallas_call | solution.py:37
  (64 shorter events, 12.8 us)
Async XLA Ops:
  6.9 82.7 %all-to-all-start = ((bf16[256,8,640]{2,1,0:T(8,128)(2,1)}), bf16[256,8,640]{2,1,0:T(8,128)(2,1)S(1)}, u32[]{:S(2)}, u32[]{:S(2)}) async-start(bf16[256,8,640]{2,1,0:T(8,128)(2,1)} %copy-done), calls=%async_computation | async-start | bytes 5242880 | tf_op jit(solution)/shard_map/all_to_all | solution.py:215
  35.6 5.4 %collective-permute-start.4 = (s32[16,256]{1,0:T(8,128)S(1)}, s32[16,256]{1,0:T(8,128)S(1)}, u32[]{:S(2)}, u32[]{:S(2)}) collective-permute-start(s32[16,256]{1,0:T(8,128)S(1)} %concatenate.22), channel_id=1, source_target_pairs={{0,16},{1,17},{2,18},{3,19},{4,20},{5,21},{6,22},{7,23},{8,24},{9,... | collective-permute-start | bytes 49160 | tf_op jit(solution)/shard_map/ppermute | solution.py:218
  41.3 37.5 %collective-permute-start.10 = (s32[8,256]{1,0:T(8,128)S(1)}, s32[8,256]{1,0:T(8,128)S(1)}, u32[]{:S(2)}, u32[]{:S(2)}) collective-permute-start(s32[8,256]{1,0:T(8,128)S(1)} %shard_map.94.refs_0_), channel_id=1, source_target_pairs={{0,192},{32,224},{64,0},{96,32},{128,64},{160,96},{192,128},{224,1... | collective-permute-start | bytes 24584 | tf_op jit(solution)/shard_map/ppermute | solution.py:177
  46.4 37.8 %collective-permute-start.11 = (s32[8,256]{1,0:T(8,128)S(1)}, s32[8,256]{1,0:T(8,128)S(1)}, u32[]{:S(2)}, u32[]{:S(2)}) collective-permute-start(s32[8,256]{1,0:T(8,128)S(1)} %shard_map.94.refs_0_), channel_id=1, source_target_pairs={{0,224},{32,0},{64,32},{96,64},{128,96},{160,128},{192,160},{224,1... | collective-permute-start | bytes 24584 | tf_op jit(solution)/shard_map/ppermute | solution.py:177
  47.8 36.4 %collective-permute-start.5 = (s32[8,256]{1,0:T(8,128)S(1)}, s32[8,256]{1,0:T(8,128)S(1)}, u32[]{:S(2)}, u32[]{:S(2)}) collective-permute-start(s32[8,256]{1,0:T(8,128)S(1)} %shard_map.94.refs_0_), channel_id=1, source_target_pairs={{0,32},{32,64},{64,96},{96,128},{128,160},{160,192},{192,224},{224... | collective-permute-start | bytes 24584 | tf_op jit(solution)/shard_map/ppermute | solution.py:177
  48.5 35.7 %collective-permute-start.6 = (s32[8,256]{1,0:T(8,128)S(1)}, s32[8,256]{1,0:T(8,128)S(1)}, u32[]{:S(2)}, u32[]{:S(2)}) collective-permute-start(s32[8,256]{1,0:T(8,128)S(1)} %shard_map.94.refs_0_), channel_id=1, source_target_pairs={{0,64},{32,96},{64,128},{96,160},{128,192},{160,224},{192,0},{224,... | collective-permute-start | bytes 24584 | tf_op jit(solution)/shard_map/ppermute | solution.py:177
  48.9 35.3 %collective-permute-start.7 = (s32[8,256]{1,0:T(8,128)S(1)}, s32[8,256]{1,0:T(8,128)S(1)}, u32[]{:S(2)}, u32[]{:S(2)}) collective-permute-start(s32[8,256]{1,0:T(8,128)S(1)} %shard_map.94.refs_0_), channel_id=1, source_target_pairs={{0,96},{32,128},{64,160},{96,192},{128,224},{160,0},{192,32},{224,... | collective-permute-start | bytes 24584 | tf_op jit(solution)/shard_map/ppermute | solution.py:177
  78.8 7.6 %collective-permute-start.8 = (s32[8,256]{1,0:T(8,128)S(1)}, s32[8,256]{1,0:T(8,128)S(1)}, u32[]{:S(2)}, u32[]{:S(2)}) collective-permute-start(s32[8,256]{1,0:T(8,128)S(1)} %shard_map.94.refs_0_), channel_id=1, source_target_pairs={{0,128},{32,160},{64,192},{96,224},{128,0},{160,32},{192,64},{224,... | collective-permute-start | bytes 24584 | tf_op jit(solution)/shard_map/ppermute | solution.py:177
  84.2 5.5 %collective-permute-start.9 = (s32[8,256]{1,0:T(8,128)S(1)}, s32[8,256]{1,0:T(8,128)S(1)}, u32[]{:S(2)}, u32[]{:S(2)}) collective-permute-start(s32[8,256]{1,0:T(8,128)S(1)} %shard_map.94.refs_0_), channel_id=1, source_target_pairs={{0,160},{32,192},{64,224},{96,0},{128,32},{160,64},{192,96},{224,1... | collective-permute-start | bytes 24584 | tf_op jit(solution)/shard_map/ppermute | solution.py:177
  97.5 19.2 %collective-permute-start.20 = (bf16[512,256]{1,0:T(8,128)(2,1)S(1)}, bf16[512,256]{1,0:T(8,128)(2,1)S(1)}, u32[]{:S(2)}, u32[]{:S(2)}) collective-permute-start(bf16[512,256]{1,0:T(8,128)(2,1)S(1)} %get-tuple-element.24.refs_5_), channel_id=1, source_target_pairs={{0,32},{32,64},{64,96},{96,128},{128,160},{160,192},{192,224},{224... | collective-permute-start | bytes 786440 | tf_op jit(solution)/shard_map/ppermute | solution.py:177
  98.8 17.9 %collective-permute-start.24 = (bf16[512,256]{1,0:T(8,128)(2,1)S(1)}, bf16[512,256]{1,0:T(8,128)(2,1)S(1)}, u32[]{:S(2)}, u32[]{:S(2)}) collective-permute-start(bf16[512,256]{1,0:T(8,128)(2,1)S(1)} %get-tuple-element.24.refs_5_), channel_id=1, source_target_pairs={{0,224},{32,0},{64,32},{96,64},{128,96},{160,128},{192,160},{224,1... | collective-permute-start | bytes 786440 | tf_op jit(solution)/shard_map/ppermute | solution.py:177
  101.9 18.0 %collective-permute-start.12 = (bf16[512,256]{1,0:T(8,128)(2,1)S(1)}, bf16[512,256]{1,0:T(8,128)(2,1)S(1)}, u32[]{:S(2)}, u32[]{:S(2)}) collective-permute-start(bf16[512,256]{1,0:T(8,128)(2,1)S(1)} %get-tuple-element.23.refs_0_), channel_id=1, source_target_pairs={{0,32},{32,64},{64,96},{96,128},{128,160},{160,192},{192,224},{224... | collective-permute-start | bytes 786440 | tf_op jit(solution)/shard_map/ppermute | solution.py:177
  101.9 18.1 %collective-permute-start.16 = (bf16[512,256]{1,0:T(8,128)(2,1)S(1)}, bf16[512,256]{1,0:T(8,128)(2,1)S(1)}, u32[]{:S(2)}, u32[]{:S(2)}) collective-permute-start(bf16[512,256]{1,0:T(8,128)(2,1)S(1)} %get-tuple-element.23.refs_0_), channel_id=1, source_target_pairs={{0,224},{32,0},{64,32},{96,64},{128,96},{160,128},{192,160},{224,1... | collective-permute-start | bytes 786440 | tf_op jit(solution)/shard_map/ppermute | solution.py:177
  105.1 9.4 %collective-permute-start.28 = (bf16[512,128]{1,0:T(8,128)(2,1)S(1)}, bf16[512,128]{1,0:T(8,128)(2,1)S(1)}, u32[]{:S(2)}, u32[]{:S(2)}) collective-permute-start(bf16[512,128]{1,0:T(8,128)(2,1)S(1)} %get-tuple-element.25.refs_10_), channel_id=1, source_target_pairs={{0,32},{32,64},{64,96},{96,128},{128,160},{160,192},{192,224},{224... | collective-permute-start | bytes 393224 | tf_op jit(solution)/shard_map/ppermute | solution.py:177
  114.5 8.7 %collective-permute-start.32 = (bf16[512,128]{1,0:T(8,128)(2,1)S(1)}, bf16[512,128]{1,0:T(8,128)(2,1)S(1)}, u32[]{:S(2)}, u32[]{:S(2)}) collective-permute-start(bf16[512,128]{1,0:T(8,128)(2,1)S(1)} %get-tuple-element.25.refs_10_), channel_id=1, source_target_pairs={{0,224},{32,0},{64,32},{96,64},{128,96},{160,128},{192,160},{224,1... | collective-permute-start | bytes 393224 | tf_op jit(solution)/shard_map/ppermute | solution.py:177
  116.7 15.4 %collective-permute-start.21 = (bf16[512,256]{1,0:T(8,128)(2,1)S(1)}, bf16[512,256]{1,0:T(8,128)(2,1)S(1)}, u32[]{:S(2)}, u32[]{:S(2)}) collective-permute-start(bf16[512,256]{1,0:T(8,128)(2,1)S(1)} %collective-permute-done.20.refs_6_), channel_id=1, source_target_pairs={{0,32},{32,64},{64,96},{96,128},{128,160},{160,192},{192,224},{224... | collective-permute-start | bytes 786440 | tf_op jit(solution)/shard_map/ppermute | solution.py:177
  116.7 16.9 %collective-permute-start.25 = (bf16[512,256]{1,0:T(8,128)(2,1)S(1)}, bf16[512,256]{1,0:T(8,128)(2,1)S(1)}, u32[]{:S(2)}, u32[]{:S(2)}) collective-permute-start(bf16[512,256]{1,0:T(8,128)(2,1)S(1)} %collective-permute-done.24.refs_7_), channel_id=1, source_target_pairs={{0,224},{32,0},{64,32},{96,64},{128,96},{160,128},{192,160},{224,1... | collective-permute-start | bytes 786440 | tf_op jit(solution)/shard_map/ppermute | solution.py:177
  119.9 15.4 %collective-permute-start.13 = (bf16[512,256]{1,0:T(8,128)(2,1)S(1)}, bf16[512,256]{1,0:T(8,128)(2,1)S(1)}, u32[]{:S(2)}, u32[]{:S(2)}) collective-permute-start(bf16[512,256]{1,0:T(8,128)(2,1)S(1)} %collective-permute-done.12.refs_1_), channel_id=1, source_target_pairs={{0,32},{32,64},{64,96},{96,128},{128,160},{160,192},{192,224},{224... | collective-permute-start | bytes 786440 | tf_op jit(solution)/shard_map/ppermute | solution.py:177
  119.9 15.7 %collective-permute-start.17 = (bf16[512,256]{1,0:T(8,128)(2,1)S(1)}, bf16[512,256]{1,0:T(8,128)(2,1)S(1)}, u32[]{:S(2)}, u32[]{:S(2)}) collective-permute-start(bf16[512,256]{1,0:T(8,128)(2,1)S(1)} %collective-permute-done.16.refs_2_), channel_id=1, source_target_pairs={{0,224},{32,0},{64,32},{96,64},{128,96},{160,128},{192,160},{224,1... | collective-permute-start | bytes 786440 | tf_op jit(solution)/shard_map/ppermute | solution.py:177
  123.2 8.4 %collective-permute-start.29 = (bf16[512,128]{1,0:T(8,128)(2,1)S(1)}, bf16[512,128]{1,0:T(8,128)(2,1)S(1)}, u32[]{:S(2)}, u32[]{:S(2)}) collective-permute-start(bf16[512,128]{1,0:T(8,128)(2,1)S(1)} %collective-permute-done.28.refs_11_), channel_id=1, source_target_pairs={{0,32},{32,64},{64,96},{96,128},{128,160},{160,192},{192,224},{224... | collective-permute-start | bytes 393224 | tf_op jit(solution)/shard_map/ppermute | solution.py:177
  131.5 7.0 %collective-permute-start.33 = (bf16[512,128]{1,0:T(8,128)(2,1)S(1)}, bf16[512,128]{1,0:T(8,128)(2,1)S(1)}, u32[]{:S(2)}, u32[]{:S(2)}) collective-permute-start(bf16[512,128]{1,0:T(8,128)(2,1)S(1)} %collective-permute-done.32.refs_12_), channel_id=1, source_target_pairs={{0,224},{32,0},{64,32},{96,64},{128,96},{160,128},{192,160},{224,1... | collective-permute-start | bytes 393224 | tf_op jit(solution)/shard_map/ppermute | solution.py:177
  132.1 14.7 %collective-permute-start.22 = (bf16[512,256]{1,0:T(8,128)(2,1)S(1)}, bf16[512,256]{1,0:T(8,128)(2,1)S(1)}, u32[]{:S(2)}, u32[]{:S(2)}) collective-permute-start(bf16[512,256]{1,0:T(8,128)(2,1)S(1)} %collective-permute-done.21.refs_8_), channel_id=1, source_target_pairs={{0,32},{32,64},{64,96},{96,128},{128,160},{160,192},{192,224},{224... | collective-permute-start | bytes 786440 | tf_op jit(solution)/shard_map/ppermute | solution.py:177
  133.6 15.3 %collective-permute-start.26 = (bf16[512,256]{1,0:T(8,128)(2,1)S(1)}, bf16[512,256]{1,0:T(8,128)(2,1)S(1)}, u32[]{:S(2)}, u32[]{:S(2)}) collective-permute-start(bf16[512,256]{1,0:T(8,128)(2,1)S(1)} %collective-permute-done.25.refs_9_), channel_id=1, source_target_pairs={{0,224},{32,0},{64,32},{96,64},{128,96},{160,128},{192,160},{224,1... | collective-permute-start | bytes 786440 | tf_op jit(solution)/shard_map/ppermute | solution.py:177
  135.3 13.7 %collective-permute-start.14 = (bf16[512,256]{1,0:T(8,128)(2,1)S(1)}, bf16[512,256]{1,0:T(8,128)(2,1)S(1)}, u32[]{:S(2)}, u32[]{:S(2)}) collective-permute-start(bf16[512,256]{1,0:T(8,128)(2,1)S(1)} %collective-permute-done.13.refs_3_), channel_id=1, source_target_pairs={{0,32},{32,64},{64,96},{96,128},{128,160},{160,192},{192,224},{224... | collective-permute-start | bytes 786440 | tf_op jit(solution)/shard_map/ppermute | solution.py:177
  135.6 16.7 %collective-permute-start.18 = (bf16[512,256]{1,0:T(8,128)(2,1)S(1)}, bf16[512,256]{1,0:T(8,128)(2,1)S(1)}, u32[]{:S(2)}, u32[]{:S(2)}) collective-permute-start(bf16[512,256]{1,0:T(8,128)(2,1)S(1)} %collective-permute-done.17.refs_4_), channel_id=1, source_target_pairs={{0,224},{32,0},{64,32},{96,64},{128,96},{160,128},{192,160},{224,1... | collective-permute-start | bytes 786440 | tf_op jit(solution)/shard_map/ppermute | solution.py:177
  138.6 8.2 %collective-permute-start.30 = (bf16[512,128]{1,0:T(8,128)(2,1)S(1)}, bf16[512,128]{1,0:T(8,128)(2,1)S(1)}, u32[]{:S(2)}, u32[]{:S(2)}) collective-permute-start(bf16[512,128]{1,0:T(8,128)(2,1)S(1)} %collective-permute-done.29.refs_13_), channel_id=1, source_target_pairs={{0,32},{32,64},{64,96},{96,128},{128,160},{160,192},{192,224},{224... | collective-permute-start | bytes 393224 | tf_op jit(solution)/shard_map/ppermute | solution.py:177
  146.7 5.7 %collective-permute-start.34 = (bf16[512,128]{1,0:T(8,128)(2,1)S(1)}, bf16[512,128]{1,0:T(8,128)(2,1)S(1)}, u32[]{:S(2)}, u32[]{:S(2)}) collective-permute-start(bf16[512,128]{1,0:T(8,128)(2,1)S(1)} %collective-permute-done.33.refs_14_), channel_id=1, source_target_pairs={{0,224},{32,0},{64,32},{96,64},{128,96},{160,128},{192,160},{224,1... | collective-permute-start | bytes 393224 | tf_op jit(solution)/shard_map/ppermute | solution.py:177
  146.8 9.0 %collective-permute-start.31 = (bf16[256,128]{1,0:T(8,128)(2,1)S(1)}, bf16[256,128]{1,0:T(8,128)(2,1)S(1)}, u32[]{:S(2)}, u32[]{:S(2)}) collective-permute-start(bf16[256,128]{1,0:T(8,128)(2,1)S(1)} %slice.28), channel_id=1, source_target_pairs={{0,32},{32,64},{64,96},{96,128},{128,160},{160,192},{192,224},{224... | collective-permute-start | bytes 196616 | tf_op jit(solution)/shard_map/ppermute | solution.py:177
  148.9 11.2 %collective-permute-start.23 = (bf16[256,256]{1,0:T(8,128)(2,1)S(1)}, bf16[256,256]{1,0:T(8,128)(2,1)S(1)}, u32[]{:S(2)}, u32[]{:S(2)}) collective-permute-start(bf16[256,256]{1,0:T(8,128)(2,1)S(1)} %slice.26), channel_id=1, source_target_pairs={{0,32},{32,64},{64,96},{96,128},{128,160},{160,192},{192,224},{224... | collective-permute-start | bytes 393224 | tf_op jit(solution)/shard_map/ppermute | solution.py:177
  149.0 11.1 %collective-permute-start.27 = (bf16[256,256]{1,0:T(8,128)(2,1)S(1)}, bf16[256,256]{1,0:T(8,128)(2,1)S(1)}, u32[]{:S(2)}, u32[]{:S(2)}) collective-permute-start(bf16[256,256]{1,0:T(8,128)(2,1)S(1)} %slice.27), channel_id=1, source_target_pairs={{0,224},{32,0},{64,32},{96,64},{128,96},{160,128},{192,160},{224,1... | collective-permute-start | bytes 393224 | tf_op jit(solution)/shard_map/ppermute | solution.py:177
  152.3 7.8 %collective-permute-start.15 = (bf16[256,256]{1,0:T(8,128)(2,1)S(1)}, bf16[256,256]{1,0:T(8,128)(2,1)S(1)}, u32[]{:S(2)}, u32[]{:S(2)}) collective-permute-start(bf16[256,256]{1,0:T(8,128)(2,1)S(1)} %slice.24), channel_id=1, source_target_pairs={{0,32},{32,64},{64,96},{96,128},{128,160},{160,192},{192,224},{224... | collective-permute-start | bytes 393224 | tf_op jit(solution)/shard_map/ppermute | solution.py:177
  152.4 7.7 %collective-permute-start.19 = (bf16[256,256]{1,0:T(8,128)(2,1)S(1)}, bf16[256,256]{1,0:T(8,128)(2,1)S(1)}, u32[]{:S(2)}, u32[]{:S(2)}) collective-permute-start(bf16[256,256]{1,0:T(8,128)(2,1)S(1)} %slice.25), channel_id=1, source_target_pairs={{0,224},{32,0},{64,32},{96,64},{128,96},{160,128},{192,160},{224,1... | collective-permute-start | bytes 393224 | tf_op jit(solution)/shard_map/ppermute | solution.py:177
  (7 other events, 20.7 us)

commit v2 on v1

--- a/solution.py
+++ b/solution.py
@@ -46,13 +46,16 @@
     return call
 
 
-def prep_kernel(count_ref, ids_ref, grads_ref, out_ref, local_ref, buf, sems, *, owners, groups, rows_own, cols):
+def prep_kernel(count_ref, ids_ref, grads_ref, out_ref, local_ref, buf, obuf, id_buf, sems, out_sems, *, owners, groups, rows_own, cols):
     slots = ids_ref.shape[1]
+    into_ids = pltpu.make_async_copy(ids_ref, id_buf, sems.at[groups])
+    into_ids.start()
     copies = [pltpu.make_async_copy(grads_ref.at[:, g * cols : (g + 1) * cols], buf.at[g], sems.at[g]) for g in range(groups)]
     for c in copies:
         c.start()
+    into_ids.wait()
     first_new = VOCAB - rows_own * owners
-    ids = ids_ref[...]
+    ids = id_buf[...]
     position = lax.broadcasted_iota(jnp.int32, (1, slots), 1)
     live = (position < count_ref[0]) & (ids >= first_new)
     local = jnp.where(live, ids - first_new, -1)
@@ -66,10 +69,16 @@
     rank = jnp.sum(earlier.astype(jnp.int32), axis=0, keepdims=True)
     place = jnp.where(live, owner * CAP + rank, -1)
     placing = (sub == jnp.broadcast_to(place, (slots, slots))).astype(jnp.bfloat16)
+    outs = []
     for g in range(groups):
         copies[g].wait()
         got = jnp.dot(placing, buf[g], preferred_element_type=jnp.float32).astype(jnp.bfloat16)
-        out_ref[g * owners : (g + 1) * owners] = got.reshape(owners, CAP, cols)
+        obuf[g] = got.reshape(owners, CAP, cols)
+        out = pltpu.make_async_copy(obuf.at[g], out_ref.at[g * owners : (g + 1) * owners], out_sems.at[g])
+        out.start()
+        outs.append(out)
+    for out in outs:
+        out.wait()
 
 
 def rows_kernel(mine_ref, local_ref, out_ref, *, rows_own):
@@ -99,17 +108,7 @@
     return new_first, new_second, master - learn_rate * update
 
 
-def adam_kernel(where_ref, tokens_ref, *refs, owners, groups, at, width, pieces, aliased):
-    codes, refs = refs[:groups], refs[groups:]
-    state, refs = refs[:3], refs[3 + (3 if aliased else 0) :]
-    outs, refs = refs[:3], refs[3:]
-    piece_refs, refs = refs[: len(pieces)], refs[len(pieces) :]
-    code_buf, b0, b1, b2, sems = refs
-    bufs = (b0, b1, b2)
-    into = [pltpu.make_async_copy(r.at[:, pl.ds(at, width)], b, sems.at[i]) for i, (r, b) in enumerate(zip(state, bufs))]
-    for c in into:
-        c.start()
-    rows_own = b0.shape[0]
+def gradient_of(where_ref, tokens_ref, codes, code_buf, owners, groups, rows_own, at, width):
     slots = owners * CAP
     z = where_ref[0]
     for k in range(groups):
@@ -122,6 +121,40 @@
         data = tokens_ref[g * owners : (g + 1) * owners, :, at : at + width].reshape(slots, width)
         part = jnp.dot(selector, data, preferred_element_type=jnp.float32)
         gradient = part if gradient is None else gradient + part
+    return gradient
+
+
+def part_of(refs, at, bufs, sems, back=False):
+    pairs = [(r.at[:, pl.ds(at, b.shape[1])], b) for r, b in zip(refs, bufs)]
+    return [pltpu.make_async_copy(*(p[::-1] if back else p), sems.at[i]) for i, p in enumerate(pairs)]
+
+
+def adam_one_kernel(where_ref, tokens_ref, *refs, owners, groups, width):
+    codes, state, refs = refs[:groups], refs[groups : groups + 3], refs[groups + 3 :]
+    om, of, os, piece_ref, code_buf, sems = refs
+    into = part_of(state, 0, (om, of, os), sems)
+    for c in into:
+        c.start()
+    gradient = gradient_of(where_ref, tokens_ref, codes, code_buf, owners, groups, om.shape[0], 0, width)
+    for c in into:
+        c.wait()
+    new_first, new_second, new_master = adam(gradient, of[...], os[...], om[...])
+    piece_ref[...] = new_master.astype(jnp.bfloat16)
+    om[...] = new_master
+    of[...] = new_first
+    os[...] = new_second
+
+
+def adam_two_kernel(where_ref, tokens_ref, *refs, owners, groups, at, width, pieces):
+    codes, state, early, refs = refs[:groups], refs[groups : groups + 3], refs[groups + 3 : groups + 6], refs[groups + 6 :]
+    outs, piece_refs, refs = refs[:3], refs[3 : 3 + len(pieces)], refs[3 + len(pieces) :]
+    code_buf, b0, b1, b2, sems, early_sems = refs
+    bufs = (b0, b1, b2)
+    into = part_of(state, at, bufs, sems)
+    over = part_of(outs, 0, early, early_sems, back=True)
+    for c in into + over:
+        c.start()
+    gradient = gradient_of(where_ref, tokens_ref, codes, code_buf, owners, groups, b0.shape[0], at, width)
     for c in into:
         c.wait()
     new_first, new_second, new_master = adam(gradient, b1[...], b2[...], b0[...])
@@ -129,14 +162,14 @@
     b0[...] = new_master
     b1[...] = new_first
     b2[...] = new_second
-    out = [pltpu.make_async_copy(b, r.at[:, pl.ds(at, width)], sems.at[i]) for i, (r, b) in enumerate(zip(outs, bufs))]
+    out = part_of(outs, at, bufs, sems, back=True)
     for c in out:
         c.start()
     done = 0
     for piece_ref, w in zip(piece_refs, pieces):
         piece_ref[...] = rounded[:, done : done + w]
         done += w
-    for c in out:
+    for c in over + out:
         c.wait()
 
 
@@ -207,11 +240,17 @@
 
     outgoing, local = kernel(
         functools.partial(prep_kernel, rows_own=rows_own, cols=cols, **sizes),
-        [pltpu.VMEM((groups * owners, CAP, cols), bf16), pltpu.VMEM((1, slots), i32)],
-        [SM, VM, HB],
-        [VM, VM],
-        scratch_shapes=[pltpu.VMEM((groups, slots, cols), bf16), pltpu.SemaphoreType.DMA((groups,))],
-    )(token_count, token_ids.reshape(1, slots), far(out_grads))
+        [pltpu.HBM((groups * owners, CAP, cols), bf16), pltpu.VMEM((1, slots), i32)],
+        [SM, HB, HB],
+        [HB, VM],
+        scratch_shapes=[
+            pltpu.VMEM((groups, slots, cols), bf16),
+            pltpu.VMEM((groups, owners, CAP, cols), bf16),
+            pltpu.VMEM((1, slots), i32),
+            pltpu.SemaphoreType.DMA((groups + 1,)),
+            pltpu.SemaphoreType.DMA((groups,)),
+        ],
+    )(token_count, far(token_ids.reshape(1, slots)), far(out_grads))
     tokens = lax.all_to_all(outgoing, ("dp", "vocab"), split_axis=0, concat_axis=0, tiled=True)
     reach = 1
     while reach < owners:
@@ -226,31 +265,32 @@
     )(mine, local)
     codes = [codes] + [shift_by(codes, k, groups) for k in range(1, groups)]
 
-    def adam_part(at, pieces, previous):
-        width = sum(pieces)
-        aliased = previous is not None
-        n_in = 2 + groups + 3
-        return kernel(
-            functools.partial(adam_kernel, at=at, width=width, pieces=pieces, aliased=aliased, **sizes),
-            [state] * 3 + [pltpu.VMEM((rows_own, w), bf16) for w in pieces],
-            [SM, VM] + [pl.BlockSpec()] * groups + [HB] * (6 if aliased else 3),
-            [HB] * 3 + [VM] * len(pieces),
-            input_output_aliases={n_in + i: i for i in range(3)} if aliased else {},
-            scratch_shapes=[pltpu.VMEM((groups, 8, slots), i32)]
-            + [pltpu.VMEM((rows_own, width), jnp.float32)] * 3
-            + [pltpu.SemaphoreType.DMA((3,))],
-        )(z, near(tokens), *codes, master_rows, first_moment, second_moment, *(map(far, previous) if aliased else ()))
-
-    *new_state, piece_a = adam_part(0, (256,), None)
-    *new_state, piece_b, piece_c = adam_part(256, (256, cols - 512), new_state)
+    cut = 256
+    rest = cols - cut
+    f32 = jnp.float32
+    *early, piece_a = kernel(
+        functools.partial(adam_one_kernel, width=cut, **sizes),
+        [pltpu.VMEM((rows_own, cut), f32)] * 3 + [pltpu.VMEM((rows_own, cut), bf16)],
+        [SM, VM] + [pl.BlockSpec()] * groups + [HB] * 3,
+        [VM] * 4,
+        scratch_shapes=[pltpu.VMEM((groups, 8, slots), i32), pltpu.SemaphoreType.DMA((3,))],
+    )(z, near(tokens), *codes, master_rows, first_moment, second_moment)
+    *new_state, piece_b = kernel(
+        functools.partial(adam_two_kernel, at=cut, width=rest, pieces=(rest,), **sizes),
+        [state] * 3 + [pltpu.VMEM((rows_own, rest), bf16)],
+        [SM, VM] + [pl.BlockSpec()] * groups + [HB] * 3 + [VM] * 3,
+        [HB] * 3 + [VM],
+        scratch_shapes=[pltpu.VMEM((groups, 8, slots), i32)]
+        + [pltpu.VMEM((rows_own, rest), f32)] * 3
+        + [pltpu.SemaphoreType.DMA((3,)), pltpu.SemaphoreType.DMA((3,))],
+    )(z, near(tokens), *codes, master_rows, first_moment, second_moment, *map(near, early))
     shape = (rows_own, cols * groups)
     got_a, last_a = ring(piece_a, 0, groups)
-    got_b, last_b = ring(piece_b, 256, groups)
-    got_c, last_c = ring(piece_c, 512, groups)
+    got_b, last_b = ring(piece_b, cut, groups)
     half = len(got_a) - 2
-    table = put(None, z, got_a[:half] + got_b[:half] + got_c[:half], shape, cols, groups)
-    table = put(table, z, got_a[half:] + got_b[half:] + got_c[half:], shape, cols, groups)
-    table = put(table, z, last_a + last_b + last_c, shape, cols, groups)
+    table = put(None, z, got_a[:half] + got_b[:half], shape, cols, groups)
+    table = put(table, z, got_a[half:] + got_b[half:], shape, cols, groups)
+    table = put(table, z, last_a + last_b, shape, cols, groups)
     return (*new_state, table)
 
 

time: 161 us -> 154 us (0.957)
  the two profiles are of different devices: /device:TPU:26 before, /device:TPU:28 now
where the time goes in v2:
time: 154 us; the launch traced here: 153 us
  waiting for transfers between devices  70.6 us (46%)
  starting transfers between devices  66.1 us (43%)
  Pallas kernels  14.9 us (10%)
  between operations  1.63 us (1%)
    ppermute x23, waiting for transfers between devices, shift_by(): return lax.ppermute(x, 'dp', [(i, (i + k) % groups) for i in range(groups)])  56.8 us
    ppermute x23, starting transfers between devices, shift_by(): return lax.ppermute(x, 'dp', [(i, (i + k) % groups) for i in range(groups)])  45.9 us
    pallas_call x7, Pallas kernels, call(): pl.pallas_call(fn, out_shape=out_shape, in_specs=in_specs, out_specs=out_...  14.9 us
    all_to_all x1, starting transfers between devices, step(): lax.all_to_all(outgoing, ('dp', 'vocab'), split_axis=0, concat_axis=0, ti...  14.4 us
    ppermute x5, waiting for transfers between devices, step(): lax.ppermute(local, 'vocab', [(i, i ^ reach) for i in range(owners)])  13.8 us
    ppermute x5, starting transfers between devices, step(): lax.ppermute(local, 'vocab', [(i, i ^ reach) for i in range(owners)])  5.74 us
  transfers between devices with their start and end apart: 29, of which 13 were waited for; matrix products, arithmetic and copies ran while one was open for 0% of the time, Pallas kernels for 2%

profile of v2, /device:TPU:28, one launch (start us, length us, event | category | flops | bytes accessed | tf_op | source)
XLA Modules:
  0.0 153.3 jit_solution(1137835939724887261)
XLA Ops:
  1.3 4.3 %shard_map.93 = (bf16[256,8,640]{2,1,0:T(8,128)(2,1)}, s32[1,256]{1,0:T(1,128)S(1)}) custom-call(s32[1]{0:T(128)S(6)} %copy.14.count_ref, s32[1,256]{1,0:T(1,128)} %bitcast.3, bf16[256,5120]{1,0:T(8,128)(2,1)} %grads_ref.1), custom_call_target="tpu_custom_call" | custom-call | tf_op jit(solution)/shard_map/pallas_call | solution.py:37
  5.6 14.4 %all-to-all-start = ((bf16[256,8,640]{2,1,0:T(8,128)(2,1)}), bf16[256,8,640]{2,1,0:T(8,128)(2,1)S(1)}, u32[]{:S(2)}, u32[]{:S(2)}) async-start(bf16[256,8,640]{2,1,0:T(8,128)(2,1)} %get-tuple-element.14), calls=%async_computation | async-start | bytes 5242880 | tf_op jit(solution)/shard_map/all_to_all | solution.py:254
  22.0 2.9 %collective-permute-done.1 = s32[2,256]{1,0:T(2,128)S(1)} collective-permute-done((s32[2,256]{1,0:T(2,128)S(1)}, s32[2,256]{1,0:T(2,128)S(1)}, u32[]{:S(2)}, u32[]{:S(2)}) %collective-permute-start.1) | collective-permute-done | bytes 2080 | tf_op jit(solution)/shard_map/ppermute | solution.py:257
  24.9 1.6 %collective-permute-start.2 = (s32[4,256]{1,0:T(4,128)S(1)}, s32[4,256]{1,0:T(4,128)S(1)}, u32[]{:S(2)}, u32[]{:S(2)}) collective-permute-start(s32[4,256]{1,0:T(4,128)S(1)} %pad_add_fusion.1), channel_id=1, source_target_pairs={{0,4},{1,5},{2,6},{3,7},{4,0},{5,1},{6,2},{7,3},{8,12},{9,13},{10,... | collective-permute-start | bytes 12296 | tf_op jit(solution)/shard_map/ppermute | solution.py:257
  26.5 3.6 %collective-permute-done.2 = s32[4,256]{1,0:T(4,128)S(1)} collective-permute-done((s32[4,256]{1,0:T(4,128)S(1)}, s32[4,256]{1,0:T(4,128)S(1)}, u32[]{:S(2)}, u32[]{:S(2)}) %collective-permute-start.2) | collective-permute-done | bytes 4128 | tf_op jit(solution)/shard_map/ppermute | solution.py:257
  30.1 1.4 collective-permute-start.3
  31.6 2.3 %collective-permute-done.3 = s32[8,256]{1,0:T(8,128)S(1)} collective-permute-done((s32[8,256]{1,0:T(8,128)S(1)}, s32[8,256]{1,0:T(8,128)S(1)}, u32[]{:S(2)}, u32[]{:S(2)}) %collective-permute-start.3) | collective-permute-done | bytes 8224 | tf_op jit(solution)/shard_map/ppermute | solution.py:257
  33.9 1.7 %collective-permute-start.4 = (s32[16,256]{1,0:T(8,128)S(1)}, s32[16,256]{1,0:T(8,128)S(1)}, u32[]{:S(2)}, u32[]{:S(2)}) collective-permute-start(s32[16,256]{1,0:T(8,128)S(1)} %concatenate.22), channel_id=1, source_target_pairs={{0,16},{1,17},{2,18},{3,19},{4,20},{5,21},{6,22},{7,23},{8,24},{9,... | collective-permute-start | bytes 49160 | tf_op jit(solution)/shard_map/ppermute | solution.py:257
  35.7 3.9 %collective-permute-done.4 = s32[16,256]{1,0:T(8,128)S(1)} collective-permute-done((s32[16,256]{1,0:T(8,128)S(1)}, s32[16,256]{1,0:T(8,128)S(1)}, u32[]{:S(2)}, u32[]{:S(2)}) %collective-permute-start.4) | collective-permute-done | bytes 16416 | tf_op jit(solution)/shard_map/ppermute | solution.py:257
  39.9 5.9 %collective-permute-start.10 = (s32[8,256]{1,0:T(8,128)S(1)}, s32[8,256]{1,0:T(8,128)S(1)}, u32[]{:S(2)}, u32[]{:S(2)}) collective-permute-start(s32[8,256]{1,0:T(8,128)S(1)} %shard_map.94.refs_0_), channel_id=1, source_target_pairs={{0,192},{32,224},{64,0},{96,32},{128,64},{160,96},{192,128},{224,1... | collective-permute-start | bytes 24584 | tf_op jit(solution)/shard_map/ppermute | solution.py:210
  45.8 1.5 collective-permute-start.11
  47.9 4.2 %collective-permute-start.7 = (s32[8,256]{1,0:T(8,128)S(1)}, s32[8,256]{1,0:T(8,128)S(1)}, u32[]{:S(2)}, u32[]{:S(2)}) collective-permute-start(s32[8,256]{1,0:T(8,128)S(1)} %shard_map.94.refs_0_), channel_id=1, source_target_pairs={{0,96},{32,128},{64,160},{96,192},{128,224},{160,0},{192,32},{224,... | collective-permute-start | bytes 24584 | tf_op jit(solution)/shard_map/ppermute | solution.py:210
  52.1 24.6 %collective-permute-done.10.refs_6_ = s32[8,256]{1,0:T(8,128)S(1)} collective-permute-done((s32[8,256]{1,0:T(8,128)S(1)}, s32[8,256]{1,0:T(8,128)S(1)}, u32[]{:S(2)}, u32[]{:S(2)}) %collective-permute-start.10) | collective-permute-done | bytes 8224 | tf_op jit(solution)/shard_map/ppermute | solution.py:210
  76.7 6.0 %collective-permute-start.8 = (s32[8,256]{1,0:T(8,128)S(1)}, s32[8,256]{1,0:T(8,128)S(1)}, u32[]{:S(2)}, u32[]{:S(2)}) collective-permute-start(s32[8,256]{1,0:T(8,128)S(1)} %shard_map.94.refs_0_), channel_id=1, source_target_pairs={{0,128},{32,160},{64,192},{96,224},{128,0},{160,32},{192,64},{224,... | collective-permute-start | bytes 24584 | tf_op jit(solution)/shard_map/ppermute | solution.py:210
  82.7 1.5 %collective-permute-done.8.refs_4_ = s32[8,256]{1,0:T(8,128)S(1)} collective-permute-done((s32[8,256]{1,0:T(8,128)S(1)}, s32[8,256]{1,0:T(8,128)S(1)}, u32[]{:S(2)}, u32[]{:S(2)}) %collective-permute-start.8) | collective-permute-done | bytes 8224 | tf_op jit(solution)/shard_map/ppermute | solution.py:210
  84.3 3.8 %collective-permute-done.9.refs_5_ = s32[8,256]{1,0:T(8,128)S(1)} collective-permute-done((s32[8,256]{1,0:T(8,128)S(1)}, s32[8,256]{1,0:T(8,128)S(1)}, u32[]{:S(2)}, u32[]{:S(2)}) %collective-permute-start.9) | collective-permute-done | bytes 8224 | tf_op jit(solution)/shard_map/ppermute | solution.py:210
  88.1 1.8 %shard_map.95 = (f32[512,256]{1,0:T(8,128)S(1)}, f32[512,256]{1,0:T(8,128)S(1)}, f32[512,256]{1,0:T(8,128)S(1)}, bf16[512,256]{1,0:T(8,128)(2,1)S(1)}) custom-call(s32[1]{0:T(128)} %bitcast.where_ref, bf16[256,8,640]{2,1,0:T(8,128)(2,1)S(1)} %all-to-all-done.tokens_ref, s32[8,256]{1,0:T(8,128)S(1)} %shard_map.94.refs_0_, ...), custom_call_target="tpu_custom_call" | custom-call | tf_op jit(solution)/shard_map/pallas_call | solution.py:37
  89.9 4.7 %shard_map.96 = (f32[512,640]{1,0:T(8,128)}, f32[512,640]{1,0:T(8,128)}, f32[512,640]{1,0:T(8,128)}, bf16[512,384]{1,0:T(8,128)(2,1)S(1)}) custom-call(s32[1]{0:T(128)} %bitcast.where_ref, bf16[256,8,640]{2,1,0:T(8,128)(2,1)S(1)} %all-to-all-done.tokens_ref, s32[8,256]{1,0:T(8,128)S(1)} %shard_map.94.refs_0_, s32[8,256]{1,0:T(8,128)S(1)} %collective-permute-done.5.refs_1_, ...), custom_call_target="tpu_custom_call" | custom-call | tf_op jit(solution)/shard_map/pallas_call | solution.py:37
  94.7 1.4 collective-permute-start.20
  96.1 3.2 %collective-permute-start.24 = (bf16[512,384]{1,0:T(8,128)(2,1)S(1)}, bf16[512,384]{1,0:T(8,128)(2,1)S(1)}, u32[]{:S(2)}, u32[]{:S(2)}) collective-permute-start(bf16[512,384]{1,0:T(8,128)(2,1)S(1)} %get-tuple-element.23.refs_5_), channel_id=1, source_target_pairs={{0,224},{32,0},{64,32},{96,64},{128,96},{160,128},{192,160},{224,1... | collective-permute-start | bytes 1179656 | tf_op jit(solution)/shard_map/ppermute | solution.py:210
  99.2 7.4 %collective-permute-done.20.refs_6_ = bf16[512,384]{1,0:T(8,128)(2,1)S(1)} collective-permute-done((bf16[512,384]{1,0:T(8,128)(2,1)S(1)}, bf16[512,384]{1,0:T(8,128)(2,1)S(1)}, u32[]{:S(2)}, u32[]{:S(2)}) %collective-permute-start.20) | collective-permute-done | bytes 393248 | tf_op jit(solution)/shard_map/ppermute | solution.py:210
  106.7 3.2 %collective-permute-start.25 = (bf16[512,384]{1,0:T(8,128)(2,1)S(1)}, bf16[512,384]{1,0:T(8,128)(2,1)S(1)}, u32[]{:S(2)}, u32[]{:S(2)}) collective-permute-start(bf16[512,384]{1,0:T(8,128)(2,1)S(1)} %collective-permute-done.24.refs_7_), channel_id=1, source_target_pairs={{0,224},{32,0},{64,32},{96,64},{128,96},{160,128},{192,160},{224,1... | collective-permute-start | bytes 1179656 | tf_op jit(solution)/shard_map/ppermute | solution.py:210
  109.9 3.2 %collective-permute-start.16 = (bf16[512,256]{1,0:T(8,128)(2,1)S(1)}, bf16[512,256]{1,0:T(8,128)(2,1)S(1)}, u32[]{:S(2)}, u32[]{:S(2)}) collective-permute-start(bf16[512,256]{1,0:T(8,128)(2,1)S(1)} %get-tuple-element.22.refs_0_), channel_id=1, source_target_pairs={{0,224},{32,0},{64,32},{96,64},{128,96},{160,128},{192,160},{224,1... | collective-permute-start | bytes 786440 | tf_op jit(solution)/shard_map/ppermute | solution.py:210
  113.1 9.0 %collective-permute-done.12.refs_1_ = bf16[512,256]{1,0:T(8,128)(2,1)S(1)} collective-permute-done((bf16[512,256]{1,0:T(8,128)(2,1)S(1)}, bf16[512,256]{1,0:T(8,128)(2,1)S(1)}, u32[]{:S(2)}, u32[]{:S(2)}) %collective-permute-start.12) | collective-permute-done | bytes 262176 | tf_op jit(solution)/shard_map/ppermute | solution.py:210
  122.2 3.2 %collective-permute-start.17 = (bf16[512,256]{1,0:T(8,128)(2,1)S(1)}, bf16[512,256]{1,0:T(8,128)(2,1)S(1)}, u32[]{:S(2)}, u32[]{:S(2)}) collective-permute-start(bf16[512,256]{1,0:T(8,128)(2,1)S(1)} %collective-permute-done.16.refs_2_), channel_id=1, source_target_pairs={{0,224},{32,0},{64,32},{96,64},{128,96},{160,128},{192,160},{224,1... | collective-permute-start | bytes 786440 | tf_op jit(solution)/shard_map/ppermute | solution.py:210
  125.4 3.2 %collective-permute-start.26 = (bf16[512,384]{1,0:T(8,128)(2,1)S(1)}, bf16[512,384]{1,0:T(8,128)(2,1)S(1)}, u32[]{:S(2)}, u32[]{:S(2)}) collective-permute-start(bf16[512,384]{1,0:T(8,128)(2,1)S(1)} %collective-permute-done.25.refs_9_), channel_id=1, source_target_pairs={{0,224},{32,0},{64,32},{96,64},{128,96},{160,128},{192,160},{224,1... | collective-permute-start | bytes 1179656 | tf_op jit(solution)/shard_map/ppermute | solution.py:210
  128.6 3.9 %collective-permute-done.13.refs_3_ = bf16[512,256]{1,0:T(8,128)(2,1)S(1)} collective-permute-done((bf16[512,256]{1,0:T(8,128)(2,1)S(1)}, bf16[512,256]{1,0:T(8,128)(2,1)S(1)}, u32[]{:S(2)}, u32[]{:S(2)}) %collective-permute-start.13) | collective-permute-done | bytes 262176 | tf_op jit(solution)/shard_map/ppermute | solution.py:210
  132.5 3.2 %collective-permute-start.18 = (bf16[512,256]{1,0:T(8,128)(2,1)S(1)}, bf16[512,256]{1,0:T(8,128)(2,1)S(1)}, u32[]{:S(2)}, u32[]{:S(2)}) collective-permute-start(bf16[512,256]{1,0:T(8,128)(2,1)S(1)} %collective-permute-done.17.refs_4_), channel_id=1, source_target_pairs={{0,224},{32,0},{64,32},{96,64},{128,96},{160,128},{192,160},{224,1... | collective-permute-start | bytes 786440 | tf_op jit(solution)/shard_map/ppermute | solution.py:210
  135.8 5.2 %collective-permute-done.22.refs_2_ = bf16[512,384]{1,0:T(8,128)(2,1)S(1)} collective-permute-done((bf16[512,384]{1,0:T(8,128)(2,1)S(1)}, bf16[512,384]{1,0:T(8,128)(2,1)S(1)}, u32[]{:S(2)}, u32[]{:S(2)}) %collective-permute-start.22) | collective-permute-done | bytes 393248 | tf_op jit(solution)/shard_map/ppermute | solution.py:210
  141.3 3.3 %collective-permute-start.27 = (bf16[256,384]{1,0:T(8,128)(2,1)S(1)}, bf16[256,384]{1,0:T(8,128)(2,1)S(1)}, u32[]{:S(2)}, u32[]{:S(2)}) collective-permute-start(bf16[256,384]{1,0:T(8,128)(2,1)S(1)} %slice.19), channel_id=1, source_target_pairs={{0,224},{32,0},{64,32},{96,64},{128,96},{160,128},{192,160},{224,1... | collective-permute-start | bytes 589832 | tf_op jit(solution)/shard_map/ppermute | solution.py:210
  146.1 3.3 %collective-permute-start.19 = (bf16[256,256]{1,0:T(8,128)(2,1)S(1)}, bf16[256,256]{1,0:T(8,128)(2,1)S(1)}, u32[]{:S(2)}, u32[]{:S(2)}) collective-permute-start(bf16[256,256]{1,0:T(8,128)(2,1)S(1)} %slice.17), channel_id=1, source_target_pairs={{0,224},{32,0},{64,32},{96,64},{128,96},{160,128},{192,160},{224,1... | collective-permute-start | bytes 393224 | tf_op jit(solution)/shard_map/ppermute | solution.py:210
  149.3 1.8 %shard_map.97.refs_4_ = bf16[512,5120]{1,0:T(8,128)(2,1)} custom-call(s32[1]{0:T(128)} %bitcast.where_ref, bf16[512,256]{1,0:T(8,128)(2,1)S(1)} %get-tuple-element.22.refs_0_, bf16[512,256]{1,0:T(8,128)(2,1)S(1)} %collective-permute-done.12.refs_1_, bf16[512,256]{1,0:T(8,128)(2,1)S(1)} %collective-permute-done.16.refs_2_, ...), custom_call_target="tpu_custom_call" | custom-call | tf_op jit(solution)/shard_map/pallas_call | solution.py:37
  (42 shorter events, 6.9 us)
Async XLA Ops:
  5.6 82.6 %all-to-all-start = ((bf16[256,8,640]{2,1,0:T(8,128)(2,1)}), bf16[256,8,640]{2,1,0:T(8,128)(2,1)S(1)}, u32[]{:S(2)}, u32[]{:S(2)}) async-start(bf16[256,8,640]{2,1,0:T(8,128)(2,1)} %get-tuple-element.14), calls=%async_computation | async-start | bytes 5242880 | tf_op jit(solution)/shard_map/all_to_all | solution.py:254
  20.0 1.2 collective-permute-start
  21.2 3.7 %collective-permute-start.1 = (s32[2,256]{1,0:T(2,128)S(1)}, s32[2,256]{1,0:T(2,128)S(1)}, u32[]{:S(2)}, u32[]{:S(2)}) collective-permute-start(s32[2,256]{1,0:T(2,128)S(1)} %pad_add_fusion.2), channel_id=1, source_target_pairs={{0,2},{1,3},{2,0},{3,1},{4,6},{5,7},{6,4},{7,5},{8,10},{9,11},{10,... | collective-permute-start | bytes 6152 | tf_op jit(solution)/shard_map/ppermute | solution.py:257
  24.9 5.2 %collective-permute-start.2 = (s32[4,256]{1,0:T(4,128)S(1)}, s32[4,256]{1,0:T(4,128)S(1)}, u32[]{:S(2)}, u32[]{:S(2)}) collective-permute-start(s32[4,256]{1,0:T(4,128)S(1)} %pad_add_fusion.1), channel_id=1, source_target_pairs={{0,4},{1,5},{2,6},{3,7},{4,0},{5,1},{6,2},{7,3},{8,12},{9,13},{10,... | collective-permute-start | bytes 12296 | tf_op jit(solution)/shard_map/ppermute | solution.py:257
  30.1 3.8 %collective-permute-start.3 = (s32[8,256]{1,0:T(8,128)S(1)}, s32[8,256]{1,0:T(8,128)S(1)}, u32[]{:S(2)}, u32[]{:S(2)}) collective-permute-start(s32[8,256]{1,0:T(8,128)S(1)} %pad_add_fusion), channel_id=1, source_target_pairs={{0,8},{1,9},{2,10},{3,11},{4,12},{5,13},{6,14},{7,15},{8,0},{9,1},... | collective-permute-start | bytes 24584 | tf_op jit(solution)/shard_map/ppermute | solution.py:257
  33.9 5.6 %collective-permute-start.4 = (s32[16,256]{1,0:T(8,128)S(1)}, s32[16,256]{1,0:T(8,128)S(1)}, u32[]{:S(2)}, u32[]{:S(2)}) collective-permute-start(s32[16,256]{1,0:T(8,128)S(1)} %concatenate.22), channel_id=1, source_target_pairs={{0,16},{1,17},{2,18},{3,19},{4,20},{5,21},{6,22},{7,23},{8,24},{9,... | collective-permute-start | bytes 49160 | tf_op jit(solution)/shard_map/ppermute | solution.py:257
  39.9 36.8 %collective-permute-start.10 = (s32[8,256]{1,0:T(8,128)S(1)}, s32[8,256]{1,0:T(8,128)S(1)}, u32[]{:S(2)}, u32[]{:S(2)}) collective-permute-start(s32[8,256]{1,0:T(8,128)S(1)} %shard_map.94.refs_0_), channel_id=1, source_target_pairs={{0,192},{32,224},{64,0},{96,32},{128,64},{160,96},{192,128},{224,1... | collective-permute-start | bytes 24584 | tf_op jit(solution)/shard_map/ppermute | solution.py:210
  45.8 36.9 %collective-permute-start.11 = (s32[8,256]{1,0:T(8,128)S(1)}, s32[8,256]{1,0:T(8,128)S(1)}, u32[]{:S(2)}, u32[]{:S(2)}) collective-permute-start(s32[8,256]{1,0:T(8,128)S(1)} %shard_map.94.refs_0_), channel_id=1, source_target_pairs={{0,224},{32,0},{64,32},{96,64},{128,96},{160,128},{192,160},{224,1... | collective-permute-start | bytes 24584 | tf_op jit(solution)/shard_map/ppermute | solution.py:210
  47.3 35.5 %collective-permute-start.5 = (s32[8,256]{1,0:T(8,128)S(1)}, s32[8,256]{1,0:T(8,128)S(1)}, u32[]{:S(2)}, u32[]{:S(2)}) collective-permute-start(s32[8,256]{1,0:T(8,128)S(1)} %shard_map.94.refs_0_), channel_id=1, source_target_pairs={{0,32},{32,64},{64,96},{96,128},{128,160},{160,192},{192,224},{224... | collective-permute-start | bytes 24584 | tf_op jit(solution)/shard_map/ppermute | solution.py:210
  47.8 34.9 %collective-permute-start.6 = (s32[8,256]{1,0:T(8,128)S(1)}, s32[8,256]{1,0:T(8,128)S(1)}, u32[]{:S(2)}, u32[]{:S(2)}) collective-permute-start(s32[8,256]{1,0:T(8,128)S(1)} %shard_map.94.refs_0_), channel_id=1, source_target_pairs={{0,64},{32,96},{64,128},{96,160},{128,192},{160,224},{192,0},{224,... | collective-permute-start | bytes 24584 | tf_op jit(solution)/shard_map/ppermute | solution.py:210
  47.9 34.8 %collective-permute-start.7 = (s32[8,256]{1,0:T(8,128)S(1)}, s32[8,256]{1,0:T(8,128)S(1)}, u32[]{:S(2)}, u32[]{:S(2)}) collective-permute-start(s32[8,256]{1,0:T(8,128)S(1)} %shard_map.94.refs_0_), channel_id=1, source_target_pairs={{0,96},{32,128},{64,160},{96,192},{128,224},{160,0},{192,32},{224,... | collective-permute-start | bytes 24584 | tf_op jit(solution)/shard_map/ppermute | solution.py:210
  76.7 7.6 %collective-permute-start.8 = (s32[8,256]{1,0:T(8,128)S(1)}, s32[8,256]{1,0:T(8,128)S(1)}, u32[]{:S(2)}, u32[]{:S(2)}) collective-permute-start(s32[8,256]{1,0:T(8,128)S(1)} %shard_map.94.refs_0_), channel_id=1, source_target_pairs={{0,128},{32,160},{64,192},{96,224},{128,0},{160,32},{192,64},{224,... | collective-permute-start | bytes 24584 | tf_op jit(solution)/shard_map/ppermute | solution.py:210
  82.7 5.5 %collective-permute-start.9 = (s32[8,256]{1,0:T(8,128)S(1)}, s32[8,256]{1,0:T(8,128)S(1)}, u32[]{:S(2)}, u32[]{:S(2)}) collective-permute-start(s32[8,256]{1,0:T(8,128)S(1)} %shard_map.94.refs_0_), channel_id=1, source_target_pairs={{0,160},{32,192},{64,224},{96,0},{128,32},{160,64},{192,96},{224,1... | collective-permute-start | bytes 24584 | tf_op jit(solution)/shard_map/ppermute | solution.py:210
  94.7 12.0 %collective-permute-start.20 = (bf16[512,384]{1,0:T(8,128)(2,1)S(1)}, bf16[512,384]{1,0:T(8,128)(2,1)S(1)}, u32[]{:S(2)}, u32[]{:S(2)}) collective-permute-start(bf16[512,384]{1,0:T(8,128)(2,1)S(1)} %get-tuple-element.23.refs_5_), channel_id=1, source_target_pairs={{0,32},{32,64},{64,96},{96,128},{128,160},{160,192},{192,224},{224... | collective-permute-start | bytes 1179656 | tf_op jit(solution)/shard_map/ppermute | solution.py:210
  96.1 10.6 %collective-permute-start.24 = (bf16[512,384]{1,0:T(8,128)(2,1)S(1)}, bf16[512,384]{1,0:T(8,128)(2,1)S(1)}, u32[]{:S(2)}, u32[]{:S(2)}) collective-permute-start(bf16[512,384]{1,0:T(8,128)(2,1)S(1)} %get-tuple-element.23.refs_5_), channel_id=1, source_target_pairs={{0,224},{32,0},{64,32},{96,64},{128,96},{160,128},{192,160},{224,1... | collective-permute-start | bytes 1179656 | tf_op jit(solution)/shard_map/ppermute | solution.py:210
  106.7 18.7 %collective-permute-start.21 = (bf16[512,384]{1,0:T(8,128)(2,1)S(1)}, bf16[512,384]{1,0:T(8,128)(2,1)S(1)}, u32[]{:S(2)}, u32[]{:S(2)}) collective-permute-start(bf16[512,384]{1,0:T(8,128)(2,1)S(1)} %collective-permute-done.20.refs_6_), channel_id=1, source_target_pairs={{0,32},{32,64},{64,96},{96,128},{128,160},{160,192},{192,224},{224... | collective-permute-start | bytes 1179656 | tf_op jit(solution)/shard_map/ppermute | solution.py:210
  106.7 18.7 %collective-permute-start.25 = (bf16[512,384]{1,0:T(8,128)(2,1)S(1)}, bf16[512,384]{1,0:T(8,128)(2,1)S(1)}, u32[]{:S(2)}, u32[]{:S(2)}) collective-permute-start(bf16[512,384]{1,0:T(8,128)(2,1)S(1)} %collective-permute-done.24.refs_7_), channel_id=1, source_target_pairs={{0,224},{32,0},{64,32},{96,64},{128,96},{160,128},{192,160},{224,1... | collective-permute-start | bytes 1179656 | tf_op jit(solution)/shard_map/ppermute | solution.py:210
  109.9 12.3 %collective-permute-start.12 = (bf16[512,256]{1,0:T(8,128)(2,1)S(1)}, bf16[512,256]{1,0:T(8,128)(2,1)S(1)}, u32[]{:S(2)}, u32[]{:S(2)}) collective-permute-start(bf16[512,256]{1,0:T(8,128)(2,1)S(1)} %get-tuple-element.22.refs_0_), channel_id=1, source_target_pairs={{0,32},{32,64},{64,96},{96,128},{128,160},{160,192},{192,224},{224... | collective-permute-start | bytes 786440 | tf_op jit(solution)/shard_map/ppermute | solution.py:210
  109.9 12.3 %collective-permute-start.16 = (bf16[512,256]{1,0:T(8,128)(2,1)S(1)}, bf16[512,256]{1,0:T(8,128)(2,1)S(1)}, u32[]{:S(2)}, u32[]{:S(2)}) collective-permute-start(bf16[512,256]{1,0:T(8,128)(2,1)S(1)} %get-tuple-element.22.refs_0_), channel_id=1, source_target_pairs={{0,224},{32,0},{64,32},{96,64},{128,96},{160,128},{192,160},{224,1... | collective-permute-start | bytes 786440 | tf_op jit(solution)/shard_map/ppermute | solution.py:210
  122.2 10.4 %collective-permute-start.13 = (bf16[512,256]{1,0:T(8,128)(2,1)S(1)}, bf16[512,256]{1,0:T(8,128)(2,1)S(1)}, u32[]{:S(2)}, u32[]{:S(2)}) collective-permute-start(bf16[512,256]{1,0:T(8,128)(2,1)S(1)} %collective-permute-done.12.refs_1_), channel_id=1, source_target_pairs={{0,32},{32,64},{64,96},{96,128},{128,160},{160,192},{192,224},{224... | collective-permute-start | bytes 786440 | tf_op jit(solution)/shard_map/ppermute | solution.py:210
  122.2 10.4 %collective-permute-start.17 = (bf16[512,256]{1,0:T(8,128)(2,1)S(1)}, bf16[512,256]{1,0:T(8,128)(2,1)S(1)}, u32[]{:S(2)}, u32[]{:S(2)}) collective-permute-start(bf16[512,256]{1,0:T(8,128)(2,1)S(1)} %collective-permute-done.16.refs_2_), channel_id=1, source_target_pairs={{0,224},{32,0},{64,32},{96,64},{128,96},{160,128},{192,160},{224,1... | collective-permute-start | bytes 786440 | tf_op jit(solution)/shard_map/ppermute | solution.py:210
  125.4 15.6 %collective-permute-start.22 = (bf16[512,384]{1,0:T(8,128)(2,1)S(1)}, bf16[512,384]{1,0:T(8,128)(2,1)S(1)}, u32[]{:S(2)}, u32[]{:S(2)}) collective-permute-start(bf16[512,384]{1,0:T(8,128)(2,1)S(1)} %collective-permute-done.21.refs_8_), channel_id=1, source_target_pairs={{0,32},{32,64},{64,96},{96,128},{128,160},{160,192},{192,224},{224... | collective-permute-start | bytes 1179656 | tf_op jit(solution)/shard_map/ppermute | solution.py:210
  125.4 15.9 %collective-permute-start.26 = (bf16[512,384]{1,0:T(8,128)(2,1)S(1)}, bf16[512,384]{1,0:T(8,128)(2,1)S(1)}, u32[]{:S(2)}, u32[]{:S(2)}) collective-permute-start(bf16[512,384]{1,0:T(8,128)(2,1)S(1)} %collective-permute-done.25.refs_9_), channel_id=1, source_target_pairs={{0,224},{32,0},{64,32},{96,64},{128,96},{160,128},{192,160},{224,1... | collective-permute-start | bytes 1179656 | tf_op jit(solution)/shard_map/ppermute | solution.py:210
  132.5 13.4 %collective-permute-start.14 = (bf16[512,256]{1,0:T(8,128)(2,1)S(1)}, bf16[512,256]{1,0:T(8,128)(2,1)S(1)}, u32[]{:S(2)}, u32[]{:S(2)}) collective-permute-start(bf16[512,256]{1,0:T(8,128)(2,1)S(1)} %collective-permute-done.13.refs_3_), channel_id=1, source_target_pairs={{0,32},{32,64},{64,96},{96,128},{128,160},{160,192},{192,224},{224... | collective-permute-start | bytes 786440 | tf_op jit(solution)/shard_map/ppermute | solution.py:210
  132.5 13.5 %collective-permute-start.18 = (bf16[512,256]{1,0:T(8,128)(2,1)S(1)}, bf16[512,256]{1,0:T(8,128)(2,1)S(1)}, u32[]{:S(2)}, u32[]{:S(2)}) collective-permute-start(bf16[512,256]{1,0:T(8,128)(2,1)S(1)} %collective-permute-done.17.refs_4_), channel_id=1, source_target_pairs={{0,224},{32,0},{64,32},{96,64},{128,96},{160,128},{192,160},{224,1... | collective-permute-start | bytes 786440 | tf_op jit(solution)/shard_map/ppermute | solution.py:210
  141.0 11.3 %collective-permute-start.23 = (bf16[256,384]{1,0:T(8,128)(2,1)S(1)}, bf16[256,384]{1,0:T(8,128)(2,1)S(1)}, u32[]{:S(2)}, u32[]{:S(2)}) collective-permute-start(bf16[256,384]{1,0:T(8,128)(2,1)S(1)} %slice.18), channel_id=1, source_target_pairs={{0,32},{32,64},{64,96},{96,128},{128,160},{160,192},{192,224},{224... | collective-permute-start | bytes 589832 | tf_op jit(solution)/shard_map/ppermute | solution.py:210
  141.3 10.9 %collective-permute-start.27 = (bf16[256,384]{1,0:T(8,128)(2,1)S(1)}, bf16[256,384]{1,0:T(8,128)(2,1)S(1)}, u32[]{:S(2)}, u32[]{:S(2)}) collective-permute-start(bf16[256,384]{1,0:T(8,128)(2,1)S(1)} %slice.19), channel_id=1, source_target_pairs={{0,224},{32,0},{64,32},{96,64},{128,96},{160,128},{192,160},{224,1... | collective-permute-start | bytes 589832 | tf_op jit(solution)/shard_map/ppermute | solution.py:210
  145.9 6.3 %collective-permute-start.15 = (bf16[256,256]{1,0:T(8,128)(2,1)S(1)}, bf16[256,256]{1,0:T(8,128)(2,1)S(1)}, u32[]{:S(2)}, u32[]{:S(2)}) collective-permute-start(bf16[256,256]{1,0:T(8,128)(2,1)S(1)} %slice.16), channel_id=1, source_target_pairs={{0,32},{32,64},{64,96},{96,128},{128,160},{160,192},{192,224},{224... | collective-permute-start | bytes 393224 | tf_op jit(solution)/shard_map/ppermute | solution.py:210
  146.1 6.2 %collective-permute-start.19 = (bf16[256,256]{1,0:T(8,128)(2,1)S(1)}, bf16[256,256]{1,0:T(8,128)(2,1)S(1)}, u32[]{:S(2)}, u32[]{:S(2)}) collective-permute-start(bf16[256,256]{1,0:T(8,128)(2,1)S(1)} %slice.17), channel_id=1, source_target_pairs={{0,224},{32,0},{64,32},{96,64},{128,96},{160,128},{192,160},{224,1... | collective-permute-start | bytes 393224 | tf_op jit(solution)/shard_map/ppermute | solution.py:210

commit v3 on v2

--- a/solution.py
+++ b/solution.py
@@ -50,7 +50,10 @@
     slots = ids_ref.shape[1]
     into_ids = pltpu.make_async_copy(ids_ref, id_buf, sems.at[groups])
     into_ids.start()
-    copies = [pltpu.make_async_copy(grads_ref.at[:, g * cols : (g + 1) * cols], buf.at[g], sems.at[g]) for g in range(groups)]
+    wide = buf.shape[2] // cols
+    copies = [
+        pltpu.make_async_copy(grads_ref.at[:, i * wide * cols : (i + 1) * wide * cols], buf.at[i], sems.at[i]) for i in range(groups // wide)
+    ]
     for c in copies:
         c.start()
     into_ids.wait()
@@ -70,13 +73,15 @@
     place = jnp.where(live, owner * CAP + rank, -1)
     placing = (sub == jnp.broadcast_to(place, (slots, slots))).astype(jnp.bfloat16)
     outs = []
-    for g in range(groups):
-        copies[g].wait()
-        got = jnp.dot(placing, buf[g], preferred_element_type=jnp.float32).astype(jnp.bfloat16)
-        obuf[g] = got.reshape(owners, CAP, cols)
-        out = pltpu.make_async_copy(obuf.at[g], out_ref.at[g * owners : (g + 1) * owners], out_sems.at[g])
-        out.start()
-        outs.append(out)
+    for i in range(groups // wide):
+        copies[i].wait()
+        got = jnp.dot(placing, buf[i], preferred_element_type=jnp.float32).astype(jnp.bfloat16)
+        for g in range(i * wide, (i + 1) * wide):
+            part = got[:, (g - i * wide) * cols : (g - i * wide + 1) * cols]
+            obuf[g] = part.reshape(owners, CAP, cols)
+            out = pltpu.make_async_copy(obuf.at[g], out_ref.at[g * owners : (g + 1) * owners], out_sems.at[g])
+            out.start()
+            outs.append(out)
     for out in outs:
         out.wait()
 
@@ -244,7 +249,7 @@
         [SM, HB, HB],
         [HB, VM],
         scratch_shapes=[
-            pltpu.VMEM((groups, slots, cols), bf16),
+            pltpu.VMEM((groups // 2, slots, 2 * cols), bf16),
             pltpu.VMEM((groups, owners, CAP, cols), bf16),
             pltpu.VMEM((1, slots), i32),
             pltpu.SemaphoreType.DMA((groups + 1,)),
@@ -265,7 +270,7 @@
     )(mine, local)
     codes = [codes] + [shift_by(codes, k, groups) for k in range(1, groups)]
 
-    cut = 256
+    cut = 384
     rest = cols - cut
     f32 = jnp.float32
     *early, piece_a = kernel(
@@ -290,7 +295,8 @@
     half = len(got_a) - 2
     table = put(None, z, got_a[:half] + got_b[:half], shape, cols, groups)
     table = put(table, z, got_a[half:] + got_b[half:], shape, cols, groups)
-    table = put(table, z, last_a + last_b, shape, cols, groups)
+    table = put(table, z, last_a, shape, cols, groups)
+    table = put(table, z, last_b, shape, cols, groups)
     return (*new_state, table)
 
 

time: 154 us -> 150 us (0.974)
  waiting for transfers between devices: 70.6 us -> 67.4 us
    ppermute x23, waiting for transfers between devices: 56.8 us -> 53.6 us  [shift_by(): return lax.ppermute(x, 'dp', [(i, (i + k) % groups) for i in range(groups)])]
    pallas_call x7 -> x8, Pallas kernels: 14.9 us -> 14.2 us  [call(): pl.pallas_call(fn, out_shape=out_shape, in_specs=in_specs, out_specs=out_...]
  transfers between devices with their start and end apart: 29 -> 29, of which waited for: 13 -> 13; matrix products, arithmetic and copies ran while one was open for 0% -> 0% of each run, Pallas kernels for 2% -> 5%
where the time goes in v3:
time: 150 us
  waiting for transfers between devices  67.4 us (45%)
  starting transfers between devices  66.2 us (44%)
  Pallas kernels  14.2 us (9%)
  between operations  1.65 us (1%)
    ppermute x23, waiting for transfers between devices, shift_by(): return lax.ppermute(x, 'dp', [(i, (i + k) % groups) for i in range(groups)])  53.6 us
    ppermute x23, starting transfers between devices, shift_by(): return lax.ppermute(x, 'dp', [(i, (i + k) % groups) for i in range(groups)])  46 us
    all_to_all x1, starting transfers between devices, step(): lax.all_to_all(outgoing, ('dp', 'vocab'), split_axis=0, concat_axis=0, ti...  14.4 us
    pallas_call x8, Pallas kernels, call(): pl.pallas_call(fn, out_shape=out_shape, in_specs=in_specs, out_specs=out_...  14.2 us
    ppermute x5, waiting for transfers between devices, step(): lax.ppermute(local, 'vocab', [(i, i ^ reach) for i in range(owners)])  13.8 us
    ppermute x5, starting transfers between devices, step(): lax.ppermute(local, 'vocab', [(i, i ^ reach) for i in range(owners)])  5.74 us
  transfers between devices with their start and end apart: 29, of which 13 were waited for; matrix products, arithmetic and copies ran while one was open for 0% of the time, Pallas kernels for 5%

profile of v3, /device:TPU:28, one launch (start us, length us, event | category | flops | bytes accessed | tf_op | source)
XLA Modules:
  0.0 149.5 jit_solution(3771135665707941839)
XLA Ops:
  1.3 3.5 %shard_map.93 = (bf16[256,8,640]{2,1,0:T(8,128)(2,1)}, s32[1,256]{1,0:T(1,128)S(1)}) custom-call(s32[1]{0:T(128)S(6)} %copy.16.count_ref, s32[1,256]{1,0:T(1,128)} %bitcast.3, bf16[256,5120]{1,0:T(8,128)(2,1)} %grads_ref.1), custom_call_target="tpu_custom_call" | custom-call | tf_op jit(solution)/shard_map/pallas_call | solution.py:37
  4.8 14.4 %all-to-all-start = ((bf16[256,8,640]{2,1,0:T(8,128)(2,1)}), bf16[256,8,640]{2,1,0:T(8,128)(2,1)S(1)}, u32[]{:S(2)}, u32[]{:S(2)}) async-start(bf16[256,8,640]{2,1,0:T(8,128)(2,1)} %get-tuple-element.14), calls=%async_computation | async-start | bytes 5242880 | tf_op jit(solution)/shard_map/all_to_all | solution.py:259
  21.3 2.9 %collective-permute-done.1 = s32[2,256]{1,0:T(2,128)S(1)} collective-permute-done((s32[2,256]{1,0:T(2,128)S(1)}, s32[2,256]{1,0:T(2,128)S(1)}, u32[]{:S(2)}, u32[]{:S(2)}) %collective-permute-start.1) | collective-permute-done | bytes 2080 | tf_op jit(solution)/shard_map/ppermute | solution.py:262
  24.2 1.6 %collective-permute-start.2 = (s32[4,256]{1,0:T(4,128)S(1)}, s32[4,256]{1,0:T(4,128)S(1)}, u32[]{:S(2)}, u32[]{:S(2)}) collective-permute-start(s32[4,256]{1,0:T(4,128)S(1)} %pad_add_fusion.1), channel_id=1, source_target_pairs={{0,4},{1,5},{2,6},{3,7},{4,0},{5,1},{6,2},{7,3},{8,12},{9,13},{10,... | collective-permute-start | bytes 12296 | tf_op jit(solution)/shard_map/ppermute | solution.py:262
  25.7 3.6 %collective-permute-done.2 = s32[4,256]{1,0:T(4,128)S(1)} collective-permute-done((s32[4,256]{1,0:T(4,128)S(1)}, s32[4,256]{1,0:T(4,128)S(1)}, u32[]{:S(2)}, u32[]{:S(2)}) %collective-permute-start.2) | collective-permute-done | bytes 4128 | tf_op jit(solution)/shard_map/ppermute | solution.py:262
  29.4 1.4 collective-permute-start.3
  30.8 2.3 %collective-permute-done.3 = s32[8,256]{1,0:T(8,128)S(1)} collective-permute-done((s32[8,256]{1,0:T(8,128)S(1)}, s32[8,256]{1,0:T(8,128)S(1)}, u32[]{:S(2)}, u32[]{:S(2)}) %collective-permute-start.3) | collective-permute-done | bytes 8224 | tf_op jit(solution)/shard_map/ppermute | solution.py:262
  33.2 1.7 %collective-permute-start.4 = (s32[16,256]{1,0:T(8,128)S(1)}, s32[16,256]{1,0:T(8,128)S(1)}, u32[]{:S(2)}, u32[]{:S(2)}) collective-permute-start(s32[16,256]{1,0:T(8,128)S(1)} %concatenate.22), channel_id=1, source_target_pairs={{0,16},{1,17},{2,18},{3,19},{4,20},{5,21},{6,22},{7,23},{8,24},{9,... | collective-permute-start | bytes 49160 | tf_op jit(solution)/shard_map/ppermute | solution.py:262
  34.9 3.9 %collective-permute-done.4 = s32[16,256]{1,0:T(8,128)S(1)} collective-permute-done((s32[16,256]{1,0:T(8,128)S(1)}, s32[16,256]{1,0:T(8,128)S(1)}, u32[]{:S(2)}, u32[]{:S(2)}) %collective-permute-start.4) | collective-permute-done | bytes 16416 | tf_op jit(solution)/shard_map/ppermute | solution.py:262
  39.1 5.9 %collective-permute-start.10 = (s32[8,256]{1,0:T(8,128)S(1)}, s32[8,256]{1,0:T(8,128)S(1)}, u32[]{:S(2)}, u32[]{:S(2)}) collective-permute-start(s32[8,256]{1,0:T(8,128)S(1)} %shard_map.94.refs_0_), channel_id=1, source_target_pairs={{0,192},{32,224},{64,0},{96,32},{128,64},{160,96},{192,128},{224,1... | collective-permute-start | bytes 24584 | tf_op jit(solution)/shard_map/ppermute | solution.py:215
  45.0 1.5 collective-permute-start.11
  47.2 4.2 %collective-permute-start.7 = (s32[8,256]{1,0:T(8,128)S(1)}, s32[8,256]{1,0:T(8,128)S(1)}, u32[]{:S(2)}, u32[]{:S(2)}) collective-permute-start(s32[8,256]{1,0:T(8,128)S(1)} %shard_map.94.refs_0_), channel_id=1, source_target_pairs={{0,96},{32,128},{64,160},{96,192},{128,224},{160,0},{192,32},{224,... | collective-permute-start | bytes 24584 | tf_op jit(solution)/shard_map/ppermute | solution.py:215
  51.4 24.6 %collective-permute-done.10.refs_6_ = s32[8,256]{1,0:T(8,128)S(1)} collective-permute-done((s32[8,256]{1,0:T(8,128)S(1)}, s32[8,256]{1,0:T(8,128)S(1)}, u32[]{:S(2)}, u32[]{:S(2)}) %collective-permute-start.10) | collective-permute-done | bytes 8224 | tf_op jit(solution)/shard_map/ppermute | solution.py:215
  76.0 6.0 %collective-permute-start.8 = (s32[8,256]{1,0:T(8,128)S(1)}, s32[8,256]{1,0:T(8,128)S(1)}, u32[]{:S(2)}, u32[]{:S(2)}) collective-permute-start(s32[8,256]{1,0:T(8,128)S(1)} %shard_map.94.refs_0_), channel_id=1, source_target_pairs={{0,128},{32,160},{64,192},{96,224},{128,0},{160,32},{192,64},{224,... | collective-permute-start | bytes 24584 | tf_op jit(solution)/shard_map/ppermute | solution.py:215
  82.0 1.5 %collective-permute-done.8.refs_4_ = s32[8,256]{1,0:T(8,128)S(1)} collective-permute-done((s32[8,256]{1,0:T(8,128)S(1)}, s32[8,256]{1,0:T(8,128)S(1)}, u32[]{:S(2)}, u32[]{:S(2)}) %collective-permute-start.8) | collective-permute-done | bytes 8224 | tf_op jit(solution)/shard_map/ppermute | solution.py:215
  83.5 3.8 %collective-permute-done.9.refs_5_ = s32[8,256]{1,0:T(8,128)S(1)} collective-permute-done((s32[8,256]{1,0:T(8,128)S(1)}, s32[8,256]{1,0:T(8,128)S(1)}, u32[]{:S(2)}, u32[]{:S(2)}) %collective-permute-start.9) | collective-permute-done | bytes 8224 | tf_op jit(solution)/shard_map/ppermute | solution.py:215
  87.4 2.2 %shard_map.95 = (f32[512,384]{1,0:T(8,128)S(1)}, f32[512,384]{1,0:T(8,128)S(1)}, f32[512,384]{1,0:T(8,128)S(1)}, bf16[512,384]{1,0:T(8,128)(2,1)S(1)}) custom-call(s32[1]{0:T(128)} %bitcast.where_ref, bf16[256,8,640]{2,1,0:T(8,128)(2,1)S(1)} %all-to-all-done.tokens_ref, s32[8,256]{1,0:T(8,128)S(1)} %shard_map.94.refs_0_, ...), custom_call_target="tpu_custom_call" | custom-call | tf_op jit(solution)/shard_map/pallas_call | solution.py:37
  91.0 3.2 %collective-permute-start.24 = (bf16[512,384]{1,0:T(8,128)(2,1)S(1)}, bf16[512,384]{1,0:T(8,128)(2,1)S(1)}, u32[]{:S(2)}, u32[]{:S(2)}) collective-permute-start(bf16[512,384]{1,0:T(8,128)(2,1)S(1)} %get-tuple-element.23.refs_0_), channel_id=1, source_target_pairs={{0,224},{32,0},{64,32},{96,64},{128,96},{160,128},{192,160},{224,1... | collective-permute-start | bytes 1179656 | tf_op jit(solution)/shard_map/ppermute | solution.py:215
  94.2 7.4 %collective-permute-done.20.refs_1_ = bf16[512,384]{1,0:T(8,128)(2,1)S(1)} collective-permute-done((bf16[512,384]{1,0:T(8,128)(2,1)S(1)}, bf16[512,384]{1,0:T(8,128)(2,1)S(1)}, u32[]{:S(2)}, u32[]{:S(2)}) %collective-permute-start.20) | collective-permute-done | bytes 393248 | tf_op jit(solution)/shard_map/ppermute | solution.py:215
  101.6 3.2 %collective-permute-start.25 = (bf16[512,384]{1,0:T(8,128)(2,1)S(1)}, bf16[512,384]{1,0:T(8,128)(2,1)S(1)}, u32[]{:S(2)}, u32[]{:S(2)}) collective-permute-start(bf16[512,384]{1,0:T(8,128)(2,1)S(1)} %collective-permute-done.24.refs_2_), channel_id=1, source_target_pairs={{0,224},{32,0},{64,32},{96,64},{128,96},{160,128},{192,160},{224,1... | collective-permute-start | bytes 1179656 | tf_op jit(solution)/shard_map/ppermute | solution.py:215
  104.8 3.8 %shard_map.96 = (f32[512,640]{1,0:T(8,128)}, f32[512,640]{1,0:T(8,128)}, f32[512,640]{1,0:T(8,128)}, bf16[512,256]{1,0:T(8,128)(2,1)S(1)}) custom-call(s32[1]{0:T(128)} %bitcast.where_ref, bf16[256,8,640]{2,1,0:T(8,128)(2,1)S(1)} %all-to-all-done.tokens_ref, s32[8,256]{1,0:T(8,128)S(1)} %shard_map.94.refs_0_, s32[8,256]{1,0:T(8,128)S(1)} %collective-permute-done.5.refs_1_, ...), custom_call_target="tpu_custom_call" | custom-call | tf_op jit(solution)/shard_map/pallas_call | solution.py:37
  108.7 3.2 %collective-permute-start.16 = (bf16[512,256]{1,0:T(8,128)(2,1)S(1)}, bf16[512,256]{1,0:T(8,128)(2,1)S(1)}, u32[]{:S(2)}, u32[]{:S(2)}) collective-permute-start(bf16[512,256]{1,0:T(8,128)(2,1)S(1)} %get-tuple-element.22.refs_5_), channel_id=1, source_target_pairs={{0,224},{32,0},{64,32},{96,64},{128,96},{160,128},{192,160},{224,1... | collective-permute-start | bytes 786440 | tf_op jit(solution)/shard_map/ppermute | solution.py:215
  112.0 5.1 %collective-permute-done.12.refs_6_ = bf16[512,256]{1,0:T(8,128)(2,1)S(1)} collective-permute-done((bf16[512,256]{1,0:T(8,128)(2,1)S(1)}, bf16[512,256]{1,0:T(8,128)(2,1)S(1)}, u32[]{:S(2)}, u32[]{:S(2)}) %collective-permute-start.12) | collective-permute-done | bytes 262176 | tf_op jit(solution)/shard_map/ppermute | solution.py:215
  117.1 3.2 %collective-permute-start.17 = (bf16[512,256]{1,0:T(8,128)(2,1)S(1)}, bf16[512,256]{1,0:T(8,128)(2,1)S(1)}, u32[]{:S(2)}, u32[]{:S(2)}) collective-permute-start(bf16[512,256]{1,0:T(8,128)(2,1)S(1)} %collective-permute-done.16.refs_7_), channel_id=1, source_target_pairs={{0,224},{32,0},{64,32},{96,64},{128,96},{160,128},{192,160},{224,1... | collective-permute-start | bytes 786440 | tf_op jit(solution)/shard_map/ppermute | solution.py:215
  120.3 3.2 %collective-permute-start.26 = (bf16[512,384]{1,0:T(8,128)(2,1)S(1)}, bf16[512,384]{1,0:T(8,128)(2,1)S(1)}, u32[]{:S(2)}, u32[]{:S(2)}) collective-permute-start(bf16[512,384]{1,0:T(8,128)(2,1)S(1)} %collective-permute-done.25.refs_4_), channel_id=1, source_target_pairs={{0,224},{32,0},{64,32},{96,64},{128,96},{160,128},{192,160},{224,1... | collective-permute-start | bytes 1179656 | tf_op jit(solution)/shard_map/ppermute | solution.py:215
  123.6 3.9 %collective-permute-done.13.refs_8_ = bf16[512,256]{1,0:T(8,128)(2,1)S(1)} collective-permute-done((bf16[512,256]{1,0:T(8,128)(2,1)S(1)}, bf16[512,256]{1,0:T(8,128)(2,1)S(1)}, u32[]{:S(2)}, u32[]{:S(2)}) %collective-permute-start.13) | collective-permute-done | bytes 262176 | tf_op jit(solution)/shard_map/ppermute | solution.py:215
  127.5 3.2 %collective-permute-start.18 = (bf16[512,256]{1,0:T(8,128)(2,1)S(1)}, bf16[512,256]{1,0:T(8,128)(2,1)S(1)}, u32[]{:S(2)}, u32[]{:S(2)}) collective-permute-start(bf16[512,256]{1,0:T(8,128)(2,1)S(1)} %collective-permute-done.17.refs_9_), channel_id=1, source_target_pairs={{0,224},{32,0},{64,32},{96,64},{128,96},{160,128},{192,160},{224,1... | collective-permute-start | bytes 786440 | tf_op jit(solution)/shard_map/ppermute | solution.py:215
  130.7 5.2 %collective-permute-done.22.refs_0_ = bf16[512,384]{1,0:T(8,128)(2,1)S(1)} collective-permute-done((bf16[512,384]{1,0:T(8,128)(2,1)S(1)}, bf16[512,384]{1,0:T(8,128)(2,1)S(1)}, u32[]{:S(2)}, u32[]{:S(2)}) %collective-permute-start.22) | collective-permute-done | bytes 393248 | tf_op jit(solution)/shard_map/ppermute | solution.py:215
  136.3 3.3 %collective-permute-start.27 = (bf16[256,384]{1,0:T(8,128)(2,1)S(1)}, bf16[256,384]{1,0:T(8,128)(2,1)S(1)}, u32[]{:S(2)}, u32[]{:S(2)}) collective-permute-start(bf16[256,384]{1,0:T(8,128)(2,1)S(1)} %slice.19), channel_id=1, source_target_pairs={{0,224},{32,0},{64,32},{96,64},{128,96},{160,128},{192,160},{224,1... | collective-permute-start | bytes 589832 | tf_op jit(solution)/shard_map/ppermute | solution.py:215
  139.6 2.0 %collective-permute-done.14.refs_2_ = bf16[512,256]{1,0:T(8,128)(2,1)S(1)} collective-permute-done((bf16[512,256]{1,0:T(8,128)(2,1)S(1)}, bf16[512,256]{1,0:T(8,128)(2,1)S(1)}, u32[]{:S(2)}, u32[]{:S(2)}) %collective-permute-start.14) | collective-permute-done | bytes 262176 | tf_op jit(solution)/shard_map/ppermute | solution.py:215
  141.6 3.3 %collective-permute-start.19 = (bf16[256,256]{1,0:T(8,128)(2,1)S(1)}, bf16[256,256]{1,0:T(8,128)(2,1)S(1)}, u32[]{:S(2)}, u32[]{:S(2)}) collective-permute-start(bf16[256,256]{1,0:T(8,128)(2,1)S(1)} %slice.17), channel_id=1, source_target_pairs={{0,224},{32,0},{64,32},{96,64},{128,96},{160,128},{192,160},{224,1... | collective-permute-start | bytes 393224 | tf_op jit(solution)/shard_map/ppermute | solution.py:215
  144.9 1.8 %shard_map.97.refs_4_ = bf16[512,5120]{1,0:T(8,128)(2,1)} custom-call(s32[1]{0:T(128)} %bitcast.where_ref, bf16[512,384]{1,0:T(8,128)(2,1)S(1)} %get-tuple-element.23.refs_0_, bf16[512,384]{1,0:T(8,128)(2,1)S(1)} %collective-permute-done.20.refs_1_, bf16[512,384]{1,0:T(8,128)(2,1)S(1)} %collective-permute-done.24.refs_2_, ...), custom_call_target="tpu_custom_call" | custom-call | tf_op jit(solution)/shard_map/pallas_call | solution.py:37
  (43 shorter events, 7.7 us)
Async XLA Ops:
  4.8 82.6 %all-to-all-start = ((bf16[256,8,640]{2,1,0:T(8,128)(2,1)}), bf16[256,8,640]{2,1,0:T(8,128)(2,1)S(1)}, u32[]{:S(2)}, u32[]{:S(2)}) async-start(bf16[256,8,640]{2,1,0:T(8,128)(2,1)} %get-tuple-element.14), calls=%async_computation | async-start | bytes 5242880 | tf_op jit(solution)/shard_map/all_to_all | solution.py:259
  19.2 1.2 collective-permute-start
  20.5 3.7 %collective-permute-start.1 = (s32[2,256]{1,0:T(2,128)S(1)}, s32[2,256]{1,0:T(2,128)S(1)}, u32[]{:S(2)}, u32[]{:S(2)}) collective-permute-start(s32[2,256]{1,0:T(2,128)S(1)} %pad_add_fusion.2), channel_id=1, source_target_pairs={{0,2},{1,3},{2,0},{3,1},{4,6},{5,7},{6,4},{7,5},{8,10},{9,11},{10,... | collective-permute-start | bytes 6152 | tf_op jit(solution)/shard_map/ppermute | solution.py:262
  24.2 5.2 %collective-permute-start.2 = (s32[4,256]{1,0:T(4,128)S(1)}, s32[4,256]{1,0:T(4,128)S(1)}, u32[]{:S(2)}, u32[]{:S(2)}) collective-permute-start(s32[4,256]{1,0:T(4,128)S(1)} %pad_add_fusion.1), channel_id=1, source_target_pairs={{0,4},{1,5},{2,6},{3,7},{4,0},{5,1},{6,2},{7,3},{8,12},{9,13},{10,... | collective-permute-start | bytes 12296 | tf_op jit(solution)/shard_map/ppermute | solution.py:262
  29.4 3.8 %collective-permute-start.3 = (s32[8,256]{1,0:T(8,128)S(1)}, s32[8,256]{1,0:T(8,128)S(1)}, u32[]{:S(2)}, u32[]{:S(2)}) collective-permute-start(s32[8,256]{1,0:T(8,128)S(1)} %pad_add_fusion), channel_id=1, source_target_pairs={{0,8},{1,9},{2,10},{3,11},{4,12},{5,13},{6,14},{7,15},{8,0},{9,1},... | collective-permute-start | bytes 24584 | tf_op jit(solution)/shard_map/ppermute | solution.py:262
  33.2 5.6 %collective-permute-start.4 = (s32[16,256]{1,0:T(8,128)S(1)}, s32[16,256]{1,0:T(8,128)S(1)}, u32[]{:S(2)}, u32[]{:S(2)}) collective-permute-start(s32[16,256]{1,0:T(8,128)S(1)} %concatenate.22), channel_id=1, source_target_pairs={{0,16},{1,17},{2,18},{3,19},{4,20},{5,21},{6,22},{7,23},{8,24},{9,... | collective-permute-start | bytes 49160 | tf_op jit(solution)/shard_map/ppermute | solution.py:262
  39.1 36.8 %collective-permute-start.10 = (s32[8,256]{1,0:T(8,128)S(1)}, s32[8,256]{1,0:T(8,128)S(1)}, u32[]{:S(2)}, u32[]{:S(2)}) collective-permute-start(s32[8,256]{1,0:T(8,128)S(1)} %shard_map.94.refs_0_), channel_id=1, source_target_pairs={{0,192},{32,224},{64,0},{96,32},{128,64},{160,96},{192,128},{224,1... | collective-permute-start | bytes 24584 | tf_op jit(solution)/shard_map/ppermute | solution.py:215
  45.0 36.9 %collective-permute-start.11 = (s32[8,256]{1,0:T(8,128)S(1)}, s32[8,256]{1,0:T(8,128)S(1)}, u32[]{:S(2)}, u32[]{:S(2)}) collective-permute-start(s32[8,256]{1,0:T(8,128)S(1)} %shard_map.94.refs_0_), channel_id=1, source_target_pairs={{0,224},{32,0},{64,32},{96,64},{128,96},{160,128},{192,160},{224,1... | collective-permute-start | bytes 24584 | tf_op jit(solution)/shard_map/ppermute | solution.py:215
  46.5 35.5 %collective-permute-start.5 = (s32[8,256]{1,0:T(8,128)S(1)}, s32[8,256]{1,0:T(8,128)S(1)}, u32[]{:S(2)}, u32[]{:S(2)}) collective-permute-start(s32[8,256]{1,0:T(8,128)S(1)} %shard_map.94.refs_0_), channel_id=1, source_target_pairs={{0,32},{32,64},{64,96},{96,128},{128,160},{160,192},{192,224},{224... | collective-permute-start | bytes 24584 | tf_op jit(solution)/shard_map/ppermute | solution.py:215
  47.1 34.9 %collective-permute-start.6 = (s32[8,256]{1,0:T(8,128)S(1)}, s32[8,256]{1,0:T(8,128)S(1)}, u32[]{:S(2)}, u32[]{:S(2)}) collective-permute-start(s32[8,256]{1,0:T(8,128)S(1)} %shard_map.94.refs_0_), channel_id=1, source_target_pairs={{0,64},{32,96},{64,128},{96,160},{128,192},{160,224},{192,0},{224,... | collective-permute-start | bytes 24584 | tf_op jit(solution)/shard_map/ppermute | solution.py:215
  47.2 34.8 %collective-permute-start.7 = (s32[8,256]{1,0:T(8,128)S(1)}, s32[8,256]{1,0:T(8,128)S(1)}, u32[]{:S(2)}, u32[]{:S(2)}) collective-permute-start(s32[8,256]{1,0:T(8,128)S(1)} %shard_map.94.refs_0_), channel_id=1, source_target_pairs={{0,96},{32,128},{64,160},{96,192},{128,224},{160,0},{192,32},{224,... | collective-permute-start | bytes 24584 | tf_op jit(solution)/shard_map/ppermute | solution.py:215
  76.0 7.6 %collective-permute-start.8 = (s32[8,256]{1,0:T(8,128)S(1)}, s32[8,256]{1,0:T(8,128)S(1)}, u32[]{:S(2)}, u32[]{:S(2)}) collective-permute-start(s32[8,256]{1,0:T(8,128)S(1)} %shard_map.94.refs_0_), channel_id=1, source_target_pairs={{0,128},{32,160},{64,192},{96,224},{128,0},{160,32},{192,64},{224,... | collective-permute-start | bytes 24584 | tf_op jit(solution)/shard_map/ppermute | solution.py:215
  81.9 5.5 %collective-permute-start.9 = (s32[8,256]{1,0:T(8,128)S(1)}, s32[8,256]{1,0:T(8,128)S(1)}, u32[]{:S(2)}, u32[]{:S(2)}) collective-permute-start(s32[8,256]{1,0:T(8,128)S(1)} %shard_map.94.refs_0_), channel_id=1, source_target_pairs={{0,160},{32,192},{64,224},{96,0},{128,32},{160,64},{192,96},{224,1... | collective-permute-start | bytes 24584 | tf_op jit(solution)/shard_map/ppermute | solution.py:215
  89.6 12.0 %collective-permute-start.20 = (bf16[512,384]{1,0:T(8,128)(2,1)S(1)}, bf16[512,384]{1,0:T(8,128)(2,1)S(1)}, u32[]{:S(2)}, u32[]{:S(2)}) collective-permute-start(bf16[512,384]{1,0:T(8,128)(2,1)S(1)} %get-tuple-element.23.refs_0_), channel_id=1, source_target_pairs={{0,32},{32,64},{64,96},{96,128},{128,160},{160,192},{192,224},{224... | collective-permute-start | bytes 1179656 | tf_op jit(solution)/shard_map/ppermute | solution.py:215
  91.0 10.6 %collective-permute-start.24 = (bf16[512,384]{1,0:T(8,128)(2,1)S(1)}, bf16[512,384]{1,0:T(8,128)(2,1)S(1)}, u32[]{:S(2)}, u32[]{:S(2)}) collective-permute-start(bf16[512,384]{1,0:T(8,128)(2,1)S(1)} %get-tuple-element.23.refs_0_), channel_id=1, source_target_pairs={{0,224},{32,0},{64,32},{96,64},{128,96},{160,128},{192,160},{224,1... | collective-permute-start | bytes 1179656 | tf_op jit(solution)/shard_map/ppermute | solution.py:215
  101.6 18.7 %collective-permute-start.21 = (bf16[512,384]{1,0:T(8,128)(2,1)S(1)}, bf16[512,384]{1,0:T(8,128)(2,1)S(1)}, u32[]{:S(2)}, u32[]{:S(2)}) collective-permute-start(bf16[512,384]{1,0:T(8,128)(2,1)S(1)} %collective-permute-done.20.refs_1_), channel_id=1, source_target_pairs={{0,32},{32,64},{64,96},{96,128},{128,160},{160,192},{192,224},{224... | collective-permute-start | bytes 1179656 | tf_op jit(solution)/shard_map/ppermute | solution.py:215
  101.6 18.7 %collective-permute-start.25 = (bf16[512,384]{1,0:T(8,128)(2,1)S(1)}, bf16[512,384]{1,0:T(8,128)(2,1)S(1)}, u32[]{:S(2)}, u32[]{:S(2)}) collective-permute-start(bf16[512,384]{1,0:T(8,128)(2,1)S(1)} %collective-permute-done.24.refs_2_), channel_id=1, source_target_pairs={{0,224},{32,0},{64,32},{96,64},{128,96},{160,128},{192,160},{224,1... | collective-permute-start | bytes 1179656 | tf_op jit(solution)/shard_map/ppermute | solution.py:215
  108.6 8.4 %collective-permute-start.12 = (bf16[512,256]{1,0:T(8,128)(2,1)S(1)}, bf16[512,256]{1,0:T(8,128)(2,1)S(1)}, u32[]{:S(2)}, u32[]{:S(2)}) collective-permute-start(bf16[512,256]{1,0:T(8,128)(2,1)S(1)} %get-tuple-element.22.refs_5_), channel_id=1, source_target_pairs={{0,32},{32,64},{64,96},{96,128},{128,160},{160,192},{192,224},{224... | collective-permute-start | bytes 786440 | tf_op jit(solution)/shard_map/ppermute | solution.py:215
  108.7 8.4 %collective-permute-start.16 = (bf16[512,256]{1,0:T(8,128)(2,1)S(1)}, bf16[512,256]{1,0:T(8,128)(2,1)S(1)}, u32[]{:S(2)}, u32[]{:S(2)}) collective-permute-start(bf16[512,256]{1,0:T(8,128)(2,1)S(1)} %get-tuple-element.22.refs_5_), channel_id=1, source_target_pairs={{0,224},{32,0},{64,32},{96,64},{128,96},{160,128},{192,160},{224,1... | collective-permute-start | bytes 786440 | tf_op jit(solution)/shard_map/ppermute | solution.py:215
  117.1 10.4 %collective-permute-start.13 = (bf16[512,256]{1,0:T(8,128)(2,1)S(1)}, bf16[512,256]{1,0:T(8,128)(2,1)S(1)}, u32[]{:S(2)}, u32[]{:S(2)}) collective-permute-start(bf16[512,256]{1,0:T(8,128)(2,1)S(1)} %collective-permute-done.12.refs_6_), channel_id=1, source_target_pairs={{0,32},{32,64},{64,96},{96,128},{128,160},{160,192},{192,224},{224... | collective-permute-start | bytes 786440 | tf_op jit(solution)/shard_map/ppermute | solution.py:215
  117.1 10.4 %collective-permute-start.17 = (bf16[512,256]{1,0:T(8,128)(2,1)S(1)}, bf16[512,256]{1,0:T(8,128)(2,1)S(1)}, u32[]{:S(2)}, u32[]{:S(2)}) collective-permute-start(bf16[512,256]{1,0:T(8,128)(2,1)S(1)} %collective-permute-done.16.refs_7_), channel_id=1, source_target_pairs={{0,224},{32,0},{64,32},{96,64},{128,96},{160,128},{192,160},{224,1... | collective-permute-start | bytes 786440 | tf_op jit(solution)/shard_map/ppermute | solution.py:215
  120.3 15.6 %collective-permute-start.22 = (bf16[512,384]{1,0:T(8,128)(2,1)S(1)}, bf16[512,384]{1,0:T(8,128)(2,1)S(1)}, u32[]{:S(2)}, u32[]{:S(2)}) collective-permute-start(bf16[512,384]{1,0:T(8,128)(2,1)S(1)} %collective-permute-done.21.refs_3_), channel_id=1, source_target_pairs={{0,32},{32,64},{64,96},{96,128},{128,160},{160,192},{192,224},{224... | collective-permute-start | bytes 1179656 | tf_op jit(solution)/shard_map/ppermute | solution.py:215
  120.3 15.9 %collective-permute-start.26 = (bf16[512,384]{1,0:T(8,128)(2,1)S(1)}, bf16[512,384]{1,0:T(8,128)(2,1)S(1)}, u32[]{:S(2)}, u32[]{:S(2)}) collective-permute-start(bf16[512,384]{1,0:T(8,128)(2,1)S(1)} %collective-permute-done.25.refs_4_), channel_id=1, source_target_pairs={{0,224},{32,0},{64,32},{96,64},{128,96},{160,128},{192,160},{224,1... | collective-permute-start | bytes 1179656 | tf_op jit(solution)/shard_map/ppermute | solution.py:215
  127.5 14.0 %collective-permute-start.14 = (bf16[512,256]{1,0:T(8,128)(2,1)S(1)}, bf16[512,256]{1,0:T(8,128)(2,1)S(1)}, u32[]{:S(2)}, u32[]{:S(2)}) collective-permute-start(bf16[512,256]{1,0:T(8,128)(2,1)S(1)} %collective-permute-done.13.refs_8_), channel_id=1, source_target_pairs={{0,32},{32,64},{64,96},{96,128},{128,160},{160,192},{192,224},{224... | collective-permute-start | bytes 786440 | tf_op jit(solution)/shard_map/ppermute | solution.py:215
  127.5 14.1 %collective-permute-start.18 = (bf16[512,256]{1,0:T(8,128)(2,1)S(1)}, bf16[512,256]{1,0:T(8,128)(2,1)S(1)}, u32[]{:S(2)}, u32[]{:S(2)}) collective-permute-start(bf16[512,256]{1,0:T(8,128)(2,1)S(1)} %collective-permute-done.17.refs_9_), channel_id=1, source_target_pairs={{0,224},{32,0},{64,32},{96,64},{128,96},{160,128},{192,160},{224,1... | collective-permute-start | bytes 786440 | tf_op jit(solution)/shard_map/ppermute | solution.py:215
  135.9 11.9 %collective-permute-start.23 = (bf16[256,384]{1,0:T(8,128)(2,1)S(1)}, bf16[256,384]{1,0:T(8,128)(2,1)S(1)}, u32[]{:S(2)}, u32[]{:S(2)}) collective-permute-start(bf16[256,384]{1,0:T(8,128)(2,1)S(1)} %slice.18), channel_id=1, source_target_pairs={{0,32},{32,64},{64,96},{96,128},{128,160},{160,192},{192,224},{224... | collective-permute-start | bytes 589832 | tf_op jit(solution)/shard_map/ppermute | solution.py:215
  136.3 11.6 %collective-permute-start.27 = (bf16[256,384]{1,0:T(8,128)(2,1)S(1)}, bf16[256,384]{1,0:T(8,128)(2,1)S(1)}, u32[]{:S(2)}, u32[]{:S(2)}) collective-permute-start(bf16[256,384]{1,0:T(8,128)(2,1)S(1)} %slice.19), channel_id=1, source_target_pairs={{0,224},{32,0},{64,32},{96,64},{128,96},{160,128},{192,160},{224,1... | collective-permute-start | bytes 589832 | tf_op jit(solution)/shard_map/ppermute | solution.py:215
  141.5 7.1 %collective-permute-start.15 = (bf16[256,256]{1,0:T(8,128)(2,1)S(1)}, bf16[256,256]{1,0:T(8,128)(2,1)S(1)}, u32[]{:S(2)}, u32[]{:S(2)}) collective-permute-start(bf16[256,256]{1,0:T(8,128)(2,1)S(1)} %slice.16), channel_id=1, source_target_pairs={{0,32},{32,64},{64,96},{96,128},{128,160},{160,192},{192,224},{224... | collective-permute-start | bytes 393224 | tf_op jit(solution)/shard_map/ppermute | solution.py:215
  141.6 7.0 %collective-permute-start.19 = (bf16[256,256]{1,0:T(8,128)(2,1)S(1)}, bf16[256,256]{1,0:T(8,128)(2,1)S(1)}, u32[]{:S(2)}, u32[]{:S(2)}) collective-permute-start(bf16[256,256]{1,0:T(8,128)(2,1)S(1)} %slice.17), channel_id=1, source_target_pairs={{0,224},{32,0},{64,32},{96,64},{128,96},{160,128},{192,160},{224,1... | collective-permute-start | bytes 393224 | tf_op jit(solution)/shard_map/ppermute | solution.py:215

commit v4 on v3

--- a/solution.py
+++ b/solution.py
@@ -113,34 +113,35 @@
     return new_first, new_second, master - learn_rate * update
 
 
-def gradient_of(where_ref, tokens_ref, codes, code_buf, owners, groups, rows_own, at, width):
+def gradient_of(where_ref, tokens_ref, codes, code_buf, owners, groups, rows, at):
     slots = owners * CAP
     z = where_ref[0]
     for k in range(groups):
         code_buf[lax.rem(z + groups - k, groups)] = codes[k][...]
-    sub = lax.broadcasted_iota(jnp.int32, (rows_own, slots), 0)
+    width = tokens_ref.shape[2]
+    sub = lax.broadcasted_iota(jnp.int32, (rows, slots), 0) + at
     gradient = None
     for g in range(groups):
-        code = jnp.broadcast_to(code_buf[g, 0:1, :], (rows_own, slots))
+        code = jnp.broadcast_to(code_buf[g, 0:1, :], (rows, slots))
         selector = (sub == code).astype(jnp.bfloat16)
-        data = tokens_ref[g * owners : (g + 1) * owners, :, at : at + width].reshape(slots, width)
+        data = tokens_ref[g * owners : (g + 1) * owners].reshape(slots, width)
         part = jnp.dot(selector, data, preferred_element_type=jnp.float32)
         gradient = part if gradient is None else gradient + part
     return gradient
 
 
 def part_of(refs, at, bufs, sems, back=False):
-    pairs = [(r.at[:, pl.ds(at, b.shape[1])], b) for r, b in zip(refs, bufs)]
+    pairs = [(r.at[pl.ds(at, b.shape[0])], b) for r, b in zip(refs, bufs)]
     return [pltpu.make_async_copy(*(p[::-1] if back else p), sems.at[i]) for i, p in enumerate(pairs)]
 
 
-def adam_one_kernel(where_ref, tokens_ref, *refs, owners, groups, width):
+def adam_one_kernel(where_ref, tokens_ref, *refs, owners, groups):
     codes, state, refs = refs[:groups], refs[groups : groups + 3], refs[groups + 3 :]
     om, of, os, piece_ref, code_buf, sems = refs
     into = part_of(state, 0, (om, of, os), sems)
     for c in into:
         c.start()
-    gradient = gradient_of(where_ref, tokens_ref, codes, code_buf, owners, groups, om.shape[0], 0, width)
+    gradient = gradient_of(where_ref, tokens_ref, codes, code_buf, owners, groups, om.shape[0], 0)
     for c in into:
         c.wait()
     new_first, new_second, new_master = adam(gradient, of[...], os[...], om[...])
@@ -150,16 +151,16 @@
     os[...] = new_second
 
 
-def adam_two_kernel(where_ref, tokens_ref, *refs, owners, groups, at, width, pieces):
+def adam_two_kernel(where_ref, tokens_ref, *refs, owners, groups, at):
     codes, state, early, refs = refs[:groups], refs[groups : groups + 3], refs[groups + 3 : groups + 6], refs[groups + 6 :]
-    outs, piece_refs, refs = refs[:3], refs[3 : 3 + len(pieces)], refs[3 + len(pieces) :]
+    outs, piece_ref, refs = refs[:3], refs[3], refs[4:]
     code_buf, b0, b1, b2, sems, early_sems = refs
     bufs = (b0, b1, b2)
     into = part_of(state, at, bufs, sems)
     over = part_of(outs, 0, early, early_sems, back=True)
     for c in into + over:
         c.start()
-    gradient = gradient_of(where_ref, tokens_ref, codes, code_buf, owners, groups, b0.shape[0], at, width)
+    gradient = gradient_of(where_ref, tokens_ref, codes, code_buf, owners, groups, b0.shape[0], at)
     for c in into:
         c.wait()
     new_first, new_second, new_master = adam(gradient, b1[...], b2[...], b0[...])
@@ -170,10 +171,7 @@
     out = part_of(outs, at, bufs, sems, back=True)
     for c in out:
         c.start()
-    done = 0
-    for piece_ref, w in zip(piece_refs, pieces):
-        piece_ref[...] = rounded[:, done : done + w]
-        done += w
+    piece_ref[...] = rounded
     for c in over + out:
         c.wait()
 
@@ -215,18 +213,18 @@
     return lax.ppermute(x, "dp", [(i, (i + k) % groups) for i in range(groups)])
 
 
-def ring(piece, off, groups):
+def ring(piece, row, groups):
     half = groups // 2
     rows = piece.shape[0]
-    got = [(piece, 0, 0, off)]
+    got = [(piece, 0, row, 0)]
     up = down = piece
     for s in range(1, half):
         up = shift_by(up, 1, groups)
         down = shift_by(down, -1, groups)
-        got += [(up, s, 0, off), (down, groups - s, 0, off)]
+        got += [(up, s, row, 0), (down, groups - s, row, 0)]
     last = [
-        (shift_by(up[: rows // 2], 1, groups), half, 0, off),
-        (shift_by(down[rows // 2 :], -1, groups), half, rows // 2, off),
+        (shift_by(up[: rows // 2], 1, groups), half, row, 0),
+        (shift_by(down[rows // 2 :], -1, groups), half, row + rows // 2, 0),
     ]
     return got, last
 
@@ -249,7 +247,7 @@
         [SM, HB, HB],
         [HB, VM],
         scratch_shapes=[
-            pltpu.VMEM((groups // 2, slots, 2 * cols), bf16),
+            pltpu.VMEM((groups // 4, slots, 4 * cols), bf16),
             pltpu.VMEM((groups, owners, CAP, cols), bf16),
             pltpu.VMEM((1, slots), i32),
             pltpu.SemaphoreType.DMA((groups + 1,)),
@@ -270,23 +268,23 @@
     )(mine, local)
     codes = [codes] + [shift_by(codes, k, groups) for k in range(1, groups)]
 
-    cut = 384
-    rest = cols - cut
+    cut = 304
+    rest = rows_own - cut
     f32 = jnp.float32
     *early, piece_a = kernel(
-        functools.partial(adam_one_kernel, width=cut, **sizes),
-        [pltpu.VMEM((rows_own, cut), f32)] * 3 + [pltpu.VMEM((rows_own, cut), bf16)],
+        functools.partial(adam_one_kernel, **sizes),
+        [pltpu.VMEM((cut, cols), f32)] * 3 + [pltpu.VMEM((cut, cols), bf16)],
         [SM, VM] + [pl.BlockSpec()] * groups + [HB] * 3,
         [VM] * 4,
         scratch_shapes=[pltpu.VMEM((groups, 8, slots), i32), pltpu.SemaphoreType.DMA((3,))],
     )(z, near(tokens), *codes, master_rows, first_moment, second_moment)
     *new_state, piece_b = kernel(
-        functools.partial(adam_two_kernel, at=cut, width=rest, pieces=(rest,), **sizes),
-        [state] * 3 + [pltpu.VMEM((rows_own, rest), bf16)],
+        functools.partial(adam_two_kernel, at=cut, **sizes),
+        [state] * 3 + [pltpu.VMEM((rest, cols), bf16)],
         [SM, VM] + [pl.BlockSpec()] * groups + [HB] * 3 + [VM] * 3,
         [HB] * 3 + [VM],
         scratch_shapes=[pltpu.VMEM((groups, 8, slots), i32)]
-        + [pltpu.VMEM((rows_own, rest), f32)] * 3
+        + [pltpu.VMEM((rest, cols), f32)] * 3
         + [pltpu.SemaphoreType.DMA((3,)), pltpu.SemaphoreType.DMA((3,))],
     )(z, near(tokens), *codes, master_rows, first_moment, second_moment, *map(near, early))
     shape = (rows_own, cols * groups)

time: 150 us -> 150 us (level)
  no operation moved by 1% of the time
where the time goes in v4:
time: 150 us
  waiting for transfers between devices  67.5 us (45%)
  starting transfers between devices  66.1 us (44%)
  Pallas kernels  14.1 us (9%)
  between operations  1.63 us (1%)
    ppermute x23, waiting for transfers between devices, shift_by(): return lax.ppermute(x, 'dp', [(i, (i + k) % groups) for i in range(groups)])  53.7 us
    ppermute x23, starting transfers between devices, shift_by(): return lax.ppermute(x, 'dp', [(i, (i + k) % groups) for i in range(groups)])  46 us
    all_to_all x1, starting transfers between devices, step(): lax.all_to_all(outgoing, ('dp', 'vocab'), split_axis=0, concat_axis=0, ti...  14.4 us
    pallas_call x8, Pallas kernels, call(): pl.pallas_call(fn, out_shape=out_shape, in_specs=in_specs, out_specs=out_...  14.1 us
    ppermute x5, waiting for transfers between devices, step(): lax.ppermute(local, 'vocab', [(i, i ^ reach) for i in range(owners)])  13.8 us
    ppermute x5, starting transfers between devices, step(): lax.ppermute(local, 'vocab', [(i, i ^ reach) for i in range(owners)])  5.74 us
  transfers between devices with their start and end apart: 29, of which 13 were waited for; matrix products, arithmetic and copies ran while one was open for 0% of the time, Pallas kernels for 5%

profile of v4, /device:TPU:28, one launch (start us, length us, event | category | flops | bytes accessed | tf_op | source)
XLA Modules:
  0.0 149.5 jit_solution(12919462331600214634)
XLA Ops:
  1.3 3.3 %shard_map.93 = (bf16[256,8,640]{2,1,0:T(8,128)(2,1)}, s32[1,256]{1,0:T(1,128)S(1)}) custom-call(s32[1]{0:T(128)S(6)} %copy.16.count_ref, s32[1,256]{1,0:T(1,128)} %bitcast.3, bf16[256,5120]{1,0:T(8,128)(2,1)} %grads_ref.1), custom_call_target="tpu_custom_call" | custom-call | tf_op jit(solution)/shard_map/pallas_call | solution.py:37
  4.6 14.4 %all-to-all-start = ((bf16[256,8,640]{2,1,0:T(8,128)(2,1)}), bf16[256,8,640]{2,1,0:T(8,128)(2,1)S(1)}, u32[]{:S(2)}, u32[]{:S(2)}) async-start(bf16[256,8,640]{2,1,0:T(8,128)(2,1)} %get-tuple-element.14), calls=%async_computation | async-start | bytes 5242880 | tf_op jit(solution)/shard_map/all_to_all | solution.py:257
  21.1 2.9 %collective-permute-done.1 = s32[2,256]{1,0:T(2,128)S(1)} collective-permute-done((s32[2,256]{1,0:T(2,128)S(1)}, s32[2,256]{1,0:T(2,128)S(1)}, u32[]{:S(2)}, u32[]{:S(2)}) %collective-permute-start.1) | collective-permute-done | bytes 2080 | tf_op jit(solution)/shard_map/ppermute | solution.py:260
  24.0 1.6 %collective-permute-start.2 = (s32[4,256]{1,0:T(4,128)S(1)}, s32[4,256]{1,0:T(4,128)S(1)}, u32[]{:S(2)}, u32[]{:S(2)}) collective-permute-start(s32[4,256]{1,0:T(4,128)S(1)} %pad_add_fusion.1), channel_id=1, source_target_pairs={{0,4},{1,5},{2,6},{3,7},{4,0},{5,1},{6,2},{7,3},{8,12},{9,13},{10,... | collective-permute-start | bytes 12296 | tf_op jit(solution)/shard_map/ppermute | solution.py:260
  25.5 3.6 %collective-permute-done.2 = s32[4,256]{1,0:T(4,128)S(1)} collective-permute-done((s32[4,256]{1,0:T(4,128)S(1)}, s32[4,256]{1,0:T(4,128)S(1)}, u32[]{:S(2)}, u32[]{:S(2)}) %collective-permute-start.2) | collective-permute-done | bytes 4128 | tf_op jit(solution)/shard_map/ppermute | solution.py:260
  30.6 2.3 %collective-permute-done.3 = s32[8,256]{1,0:T(8,128)S(1)} collective-permute-done((s32[8,256]{1,0:T(8,128)S(1)}, s32[8,256]{1,0:T(8,128)S(1)}, u32[]{:S(2)}, u32[]{:S(2)}) %collective-permute-start.3) | collective-permute-done | bytes 8224 | tf_op jit(solution)/shard_map/ppermute | solution.py:260
  33.0 1.7 %collective-permute-start.4 = (s32[16,256]{1,0:T(8,128)S(1)}, s32[16,256]{1,0:T(8,128)S(1)}, u32[]{:S(2)}, u32[]{:S(2)}) collective-permute-start(s32[16,256]{1,0:T(8,128)S(1)} %concatenate.22), channel_id=1, source_target_pairs={{0,16},{1,17},{2,18},{3,19},{4,20},{5,21},{6,22},{7,23},{8,24},{9,... | collective-permute-start | bytes 49160 | tf_op jit(solution)/shard_map/ppermute | solution.py:260
  34.7 3.9 %collective-permute-done.4 = s32[16,256]{1,0:T(8,128)S(1)} collective-permute-done((s32[16,256]{1,0:T(8,128)S(1)}, s32[16,256]{1,0:T(8,128)S(1)}, u32[]{:S(2)}, u32[]{:S(2)}) %collective-permute-start.4) | collective-permute-done | bytes 16416 | tf_op jit(solution)/shard_map/ppermute | solution.py:260
  39.0 5.9 %collective-permute-start.10 = (s32[8,256]{1,0:T(8,128)S(1)}, s32[8,256]{1,0:T(8,128)S(1)}, u32[]{:S(2)}, u32[]{:S(2)}) collective-permute-start(s32[8,256]{1,0:T(8,128)S(1)} %shard_map.94.refs_0_), channel_id=1, source_target_pairs={{0,192},{32,224},{64,0},{96,32},{128,64},{160,96},{192,128},{224,1... | collective-permute-start | bytes 24584 | tf_op jit(solution)/shard_map/ppermute | solution.py:213
  44.9 1.5 collective-permute-start.11
  47.0 4.2 %collective-permute-start.7 = (s32[8,256]{1,0:T(8,128)S(1)}, s32[8,256]{1,0:T(8,128)S(1)}, u32[]{:S(2)}, u32[]{:S(2)}) collective-permute-start(s32[8,256]{1,0:T(8,128)S(1)} %shard_map.94.refs_0_), channel_id=1, source_target_pairs={{0,96},{32,128},{64,160},{96,192},{128,224},{160,0},{192,32},{224,... | collective-permute-start | bytes 24584 | tf_op jit(solution)/shard_map/ppermute | solution.py:213
  51.2 24.6 %collective-permute-done.10.refs_6_ = s32[8,256]{1,0:T(8,128)S(1)} collective-permute-done((s32[8,256]{1,0:T(8,128)S(1)}, s32[8,256]{1,0:T(8,128)S(1)}, u32[]{:S(2)}, u32[]{:S(2)}) %collective-permute-start.10) | collective-permute-done | bytes 8224 | tf_op jit(solution)/shard_map/ppermute | solution.py:213
  75.8 6.0 %collective-permute-start.8 = (s32[8,256]{1,0:T(8,128)S(1)}, s32[8,256]{1,0:T(8,128)S(1)}, u32[]{:S(2)}, u32[]{:S(2)}) collective-permute-start(s32[8,256]{1,0:T(8,128)S(1)} %shard_map.94.refs_0_), channel_id=1, source_target_pairs={{0,128},{32,160},{64,192},{96,224},{128,0},{160,32},{192,64},{224,... | collective-permute-start | bytes 24584 | tf_op jit(solution)/shard_map/ppermute | solution.py:213
  81.8 1.5 %collective-permute-done.8.refs_4_ = s32[8,256]{1,0:T(8,128)S(1)} collective-permute-done((s32[8,256]{1,0:T(8,128)S(1)}, s32[8,256]{1,0:T(8,128)S(1)}, u32[]{:S(2)}, u32[]{:S(2)}) %collective-permute-start.8) | collective-permute-done | bytes 8224 | tf_op jit(solution)/shard_map/ppermute | solution.py:213
  83.4 3.8 %collective-permute-done.9.refs_5_ = s32[8,256]{1,0:T(8,128)S(1)} collective-permute-done((s32[8,256]{1,0:T(8,128)S(1)}, s32[8,256]{1,0:T(8,128)S(1)}, u32[]{:S(2)}, u32[]{:S(2)}) %collective-permute-start.9) | collective-permute-done | bytes 8224 | tf_op jit(solution)/shard_map/ppermute | solution.py:213
  87.2 2.2 %shard_map.95 = (f32[304,640]{1,0:T(8,128)S(1)}, f32[304,640]{1,0:T(8,128)S(1)}, f32[304,640]{1,0:T(8,128)S(1)}, bf16[304,640]{1,0:T(8,128)(2,1)S(1)}) custom-call(s32[1]{0:T(128)} %bitcast.where_ref, bf16[256,8,640]{2,1,0:T(8,128)(2,1)S(1)} %all-to-all-done.tokens_ref, s32[8,256]{1,0:T(8,128)S(1)} %shard_map.94.refs_0_, ...), custom_call_target="tpu_custom_call" | custom-call | tf_op jit(solution)/shard_map/pallas_call | solution.py:37
  89.4 1.6 %collective-permute-start.20 = (bf16[304,640]{1,0:T(8,128)(2,1)S(1)}, bf16[304,640]{1,0:T(8,128)(2,1)S(1)}, u32[]{:S(2)}, u32[]{:S(2)}) collective-permute-start(bf16[304,640]{1,0:T(8,128)(2,1)S(1)} %get-tuple-element.23.refs_0_), channel_id=1, source_target_pairs={{0,32},{32,64},{64,96},{96,128},{128,160},{160,192},{192,224},{224... | collective-permute-start | bytes 1167368 | tf_op jit(solution)/shard_map/ppermute | solution.py:213
  91.0 3.2 %collective-permute-start.24 = (bf16[304,640]{1,0:T(8,128)(2,1)S(1)}, bf16[304,640]{1,0:T(8,128)(2,1)S(1)}, u32[]{:S(2)}, u32[]{:S(2)}) collective-permute-start(bf16[304,640]{1,0:T(8,128)(2,1)S(1)} %get-tuple-element.23.refs_0_), channel_id=1, source_target_pairs={{0,224},{32,0},{64,32},{96,64},{128,96},{160,128},{192,160},{224,1... | collective-permute-start | bytes 1167368 | tf_op jit(solution)/shard_map/ppermute | solution.py:213
  94.2 7.3 %collective-permute-done.20.refs_1_ = bf16[304,640]{1,0:T(8,128)(2,1)S(1)} collective-permute-done((bf16[304,640]{1,0:T(8,128)(2,1)S(1)}, bf16[304,640]{1,0:T(8,128)(2,1)S(1)}, u32[]{:S(2)}, u32[]{:S(2)}) %collective-permute-start.20) | collective-permute-done | bytes 389152 | tf_op jit(solution)/shard_map/ppermute | solution.py:213
  101.5 3.2 %collective-permute-start.25 = (bf16[304,640]{1,0:T(8,128)(2,1)S(1)}, bf16[304,640]{1,0:T(8,128)(2,1)S(1)}, u32[]{:S(2)}, u32[]{:S(2)}) collective-permute-start(bf16[304,640]{1,0:T(8,128)(2,1)S(1)} %collective-permute-done.24.refs_2_), channel_id=1, source_target_pairs={{0,224},{32,0},{64,32},{96,64},{128,96},{160,128},{192,160},{224,1... | collective-permute-start | bytes 1167368 | tf_op jit(solution)/shard_map/ppermute | solution.py:213
  104.7 3.9 %shard_map.96 = (f32[512,640]{1,0:T(8,128)}, f32[512,640]{1,0:T(8,128)}, f32[512,640]{1,0:T(8,128)}, bf16[208,640]{1,0:T(8,128)(2,1)S(1)}) custom-call(s32[1]{0:T(128)} %bitcast.where_ref, bf16[256,8,640]{2,1,0:T(8,128)(2,1)S(1)} %all-to-all-done.tokens_ref, s32[8,256]{1,0:T(8,128)S(1)} %shard_map.94.refs_0_, s32[8,256]{1,0:T(8,128)S(1)} %collective-permute-done.5.refs_1_, ...), custom_call_target="tpu_custom_call" | custom-call | tf_op jit(solution)/shard_map/pallas_call | solution.py:37
  108.7 3.2 %collective-permute-start.16 = (bf16[208,640]{1,0:T(8,128)(2,1)S(1)}, bf16[208,640]{1,0:T(8,128)(2,1)S(1)}, u32[]{:S(2)}, u32[]{:S(2)}) collective-permute-start(bf16[208,640]{1,0:T(8,128)(2,1)S(1)} %get-tuple-element.22.refs_5_), channel_id=1, source_target_pairs={{0,224},{32,0},{64,32},{96,64},{128,96},{160,128},{192,160},{224,1... | collective-permute-start | bytes 798728 | tf_op jit(solution)/shard_map/ppermute | solution.py:213
  111.9 5.1 %collective-permute-done.12.refs_6_ = bf16[208,640]{1,0:T(8,128)(2,1)S(1)} collective-permute-done((bf16[208,640]{1,0:T(8,128)(2,1)S(1)}, bf16[208,640]{1,0:T(8,128)(2,1)S(1)}, u32[]{:S(2)}, u32[]{:S(2)}) %collective-permute-start.12) | collective-permute-done | bytes 266272 | tf_op jit(solution)/shard_map/ppermute | solution.py:213
  117.0 3.2 %collective-permute-start.17 = (bf16[208,640]{1,0:T(8,128)(2,1)S(1)}, bf16[208,640]{1,0:T(8,128)(2,1)S(1)}, u32[]{:S(2)}, u32[]{:S(2)}) collective-permute-start(bf16[208,640]{1,0:T(8,128)(2,1)S(1)} %collective-permute-done.16.refs_7_), channel_id=1, source_target_pairs={{0,224},{32,0},{64,32},{96,64},{128,96},{160,128},{192,160},{224,1... | collective-permute-start | bytes 798728 | tf_op jit(solution)/shard_map/ppermute | solution.py:213
  120.3 3.2 %collective-permute-start.26 = (bf16[304,640]{1,0:T(8,128)(2,1)S(1)}, bf16[304,640]{1,0:T(8,128)(2,1)S(1)}, u32[]{:S(2)}, u32[]{:S(2)}) collective-permute-start(bf16[304,640]{1,0:T(8,128)(2,1)S(1)} %collective-permute-done.25.refs_4_), channel_id=1, source_target_pairs={{0,224},{32,0},{64,32},{96,64},{128,96},{160,128},{192,160},{224,1... | collective-permute-start | bytes 1167368 | tf_op jit(solution)/shard_map/ppermute | solution.py:213
  123.5 4.0 %collective-permute-done.13.refs_8_ = bf16[208,640]{1,0:T(8,128)(2,1)S(1)} collective-permute-done((bf16[208,640]{1,0:T(8,128)(2,1)S(1)}, bf16[208,640]{1,0:T(8,128)(2,1)S(1)}, u32[]{:S(2)}, u32[]{:S(2)}) %collective-permute-start.13) | collective-permute-done | bytes 266272 | tf_op jit(solution)/shard_map/ppermute | solution.py:213
  127.5 3.2 %collective-permute-start.18 = (bf16[208,640]{1,0:T(8,128)(2,1)S(1)}, bf16[208,640]{1,0:T(8,128)(2,1)S(1)}, u32[]{:S(2)}, u32[]{:S(2)}) collective-permute-start(bf16[208,640]{1,0:T(8,128)(2,1)S(1)} %collective-permute-done.17.refs_9_), channel_id=1, source_target_pairs={{0,224},{32,0},{64,32},{96,64},{128,96},{160,128},{192,160},{224,1... | collective-permute-start | bytes 798728 | tf_op jit(solution)/shard_map/ppermute | solution.py:213
  130.7 5.1 %collective-permute-done.22.refs_0_ = bf16[304,640]{1,0:T(8,128)(2,1)S(1)} collective-permute-done((bf16[304,640]{1,0:T(8,128)(2,1)S(1)}, bf16[304,640]{1,0:T(8,128)(2,1)S(1)}, u32[]{:S(2)}, u32[]{:S(2)}) %collective-permute-start.22) | collective-permute-done | bytes 389152 | tf_op jit(solution)/shard_map/ppermute | solution.py:213
  136.0 3.3 %collective-permute-start.27 = (bf16[152,640]{1,0:T(8,128)(2,1)S(1)}, bf16[152,640]{1,0:T(8,128)(2,1)S(1)}, u32[]{:S(2)}, u32[]{:S(2)}) collective-permute-start(bf16[152,640]{1,0:T(8,128)(2,1)S(1)} %slice.19), channel_id=1, source_target_pairs={{0,224},{32,0},{64,32},{96,64},{128,96},{160,128},{192,160},{224,1... | collective-permute-start | bytes 583688 | tf_op jit(solution)/shard_map/ppermute | solution.py:213
  139.3 2.3 %collective-permute-done.14.refs_2_ = bf16[208,640]{1,0:T(8,128)(2,1)S(1)} collective-permute-done((bf16[208,640]{1,0:T(8,128)(2,1)S(1)}, bf16[208,640]{1,0:T(8,128)(2,1)S(1)}, u32[]{:S(2)}, u32[]{:S(2)}) %collective-permute-start.14) | collective-permute-done | bytes 266272 | tf_op jit(solution)/shard_map/ppermute | solution.py:213
  141.7 3.3 %collective-permute-start.19 = (bf16[104,640]{1,0:T(8,128)(2,1)S(1)}, bf16[104,640]{1,0:T(8,128)(2,1)S(1)}, u32[]{:S(2)}, u32[]{:S(2)}) collective-permute-start(bf16[104,640]{1,0:T(8,128)(2,1)S(1)} %slice.17), channel_id=1, source_target_pairs={{0,224},{32,0},{64,32},{96,64},{128,96},{160,128},{192,160},{224,1... | collective-permute-start | bytes 399368 | tf_op jit(solution)/shard_map/ppermute | solution.py:213
  144.9 1.8 %shard_map.97.refs_4_ = bf16[512,5120]{1,0:T(8,128)(2,1)} custom-call(s32[1]{0:T(128)} %bitcast.where_ref, bf16[304,640]{1,0:T(8,128)(2,1)S(1)} %get-tuple-element.23.refs_0_, bf16[304,640]{1,0:T(8,128)(2,1)S(1)} %collective-permute-done.20.refs_1_, bf16[304,640]{1,0:T(8,128)(2,1)S(1)} %collective-permute-done.24.refs_2_, ...), custom_call_target="tpu_custom_call" | custom-call | tf_op jit(solution)/shard_map/pallas_call | solution.py:37
  (43 shorter events, 7.5 us)
Async XLA Ops:
  4.6 82.6 %all-to-all-start = ((bf16[256,8,640]{2,1,0:T(8,128)(2,1)}), bf16[256,8,640]{2,1,0:T(8,128)(2,1)S(1)}, u32[]{:S(2)}, u32[]{:S(2)}) async-start(bf16[256,8,640]{2,1,0:T(8,128)(2,1)} %get-tuple-element.14), calls=%async_computation | async-start | bytes 5242880 | tf_op jit(solution)/shard_map/all_to_all | solution.py:257
  19.0 1.2 collective-permute-start
  20.3 3.7 %collective-permute-start.1 = (s32[2,256]{1,0:T(2,128)S(1)}, s32[2,256]{1,0:T(2,128)S(1)}, u32[]{:S(2)}, u32[]{:S(2)}) collective-permute-start(s32[2,256]{1,0:T(2,128)S(1)} %pad_add_fusion.2), channel_id=1, source_target_pairs={{0,2},{1,3},{2,0},{3,1},{4,6},{5,7},{6,4},{7,5},{8,10},{9,11},{10,... | collective-permute-start | bytes 6152 | tf_op jit(solution)/shard_map/ppermute | solution.py:260
  24.0 5.2 %collective-permute-start.2 = (s32[4,256]{1,0:T(4,128)S(1)}, s32[4,256]{1,0:T(4,128)S(1)}, u32[]{:S(2)}, u32[]{:S(2)}) collective-permute-start(s32[4,256]{1,0:T(4,128)S(1)} %pad_add_fusion.1), channel_id=1, source_target_pairs={{0,4},{1,5},{2,6},{3,7},{4,0},{5,1},{6,2},{7,3},{8,12},{9,13},{10,... | collective-permute-start | bytes 12296 | tf_op jit(solution)/shard_map/ppermute | solution.py:260
  29.2 3.8 %collective-permute-start.3 = (s32[8,256]{1,0:T(8,128)S(1)}, s32[8,256]{1,0:T(8,128)S(1)}, u32[]{:S(2)}, u32[]{:S(2)}) collective-permute-start(s32[8,256]{1,0:T(8,128)S(1)} %pad_add_fusion), channel_id=1, source_target_pairs={{0,8},{1,9},{2,10},{3,11},{4,12},{5,13},{6,14},{7,15},{8,0},{9,1},... | collective-permute-start | bytes 24584 | tf_op jit(solution)/shard_map/ppermute | solution.py:260
  33.0 5.6 %collective-permute-start.4 = (s32[16,256]{1,0:T(8,128)S(1)}, s32[16,256]{1,0:T(8,128)S(1)}, u32[]{:S(2)}, u32[]{:S(2)}) collective-permute-start(s32[16,256]{1,0:T(8,128)S(1)} %concatenate.22), channel_id=1, source_target_pairs={{0,16},{1,17},{2,18},{3,19},{4,20},{5,21},{6,22},{7,23},{8,24},{9,... | collective-permute-start | bytes 49160 | tf_op jit(solution)/shard_map/ppermute | solution.py:260
  39.0 36.8 %collective-permute-start.10 = (s32[8,256]{1,0:T(8,128)S(1)}, s32[8,256]{1,0:T(8,128)S(1)}, u32[]{:S(2)}, u32[]{:S(2)}) collective-permute-start(s32[8,256]{1,0:T(8,128)S(1)} %shard_map.94.refs_0_), channel_id=1, source_target_pairs={{0,192},{32,224},{64,0},{96,32},{128,64},{160,96},{192,128},{224,1... | collective-permute-start | bytes 24584 | tf_op jit(solution)/shard_map/ppermute | solution.py:213
  44.9 36.9 %collective-permute-start.11 = (s32[8,256]{1,0:T(8,128)S(1)}, s32[8,256]{1,0:T(8,128)S(1)}, u32[]{:S(2)}, u32[]{:S(2)}) collective-permute-start(s32[8,256]{1,0:T(8,128)S(1)} %shard_map.94.refs_0_), channel_id=1, source_target_pairs={{0,224},{32,0},{64,32},{96,64},{128,96},{160,128},{192,160},{224,1... | collective-permute-start | bytes 24584 | tf_op jit(solution)/shard_map/ppermute | solution.py:213
  46.3 35.5 %collective-permute-start.5 = (s32[8,256]{1,0:T(8,128)S(1)}, s32[8,256]{1,0:T(8,128)S(1)}, u32[]{:S(2)}, u32[]{:S(2)}) collective-permute-start(s32[8,256]{1,0:T(8,128)S(1)} %shard_map.94.refs_0_), channel_id=1, source_target_pairs={{0,32},{32,64},{64,96},{96,128},{128,160},{160,192},{192,224},{224... | collective-permute-start | bytes 24584 | tf_op jit(solution)/shard_map/ppermute | solution.py:213
  46.9 34.9 %collective-permute-start.6 = (s32[8,256]{1,0:T(8,128)S(1)}, s32[8,256]{1,0:T(8,128)S(1)}, u32[]{:S(2)}, u32[]{:S(2)}) collective-permute-start(s32[8,256]{1,0:T(8,128)S(1)} %shard_map.94.refs_0_), channel_id=1, source_target_pairs={{0,64},{32,96},{64,128},{96,160},{128,192},{160,224},{192,0},{224,... | collective-permute-start | bytes 24584 | tf_op jit(solution)/shard_map/ppermute | solution.py:213
  47.0 34.8 %collective-permute-start.7 = (s32[8,256]{1,0:T(8,128)S(1)}, s32[8,256]{1,0:T(8,128)S(1)}, u32[]{:S(2)}, u32[]{:S(2)}) collective-permute-start(s32[8,256]{1,0:T(8,128)S(1)} %shard_map.94.refs_0_), channel_id=1, source_target_pairs={{0,96},{32,128},{64,160},{96,192},{128,224},{160,0},{192,32},{224,... | collective-permute-start | bytes 24584 | tf_op jit(solution)/shard_map/ppermute | solution.py:213
  75.8 7.6 %collective-permute-start.8 = (s32[8,256]{1,0:T(8,128)S(1)}, s32[8,256]{1,0:T(8,128)S(1)}, u32[]{:S(2)}, u32[]{:S(2)}) collective-permute-start(s32[8,256]{1,0:T(8,128)S(1)} %shard_map.94.refs_0_), channel_id=1, source_target_pairs={{0,128},{32,160},{64,192},{96,224},{128,0},{160,32},{192,64},{224,... | collective-permute-start | bytes 24584 | tf_op jit(solution)/shard_map/ppermute | solution.py:213
  81.7 5.4 %collective-permute-start.9 = (s32[8,256]{1,0:T(8,128)S(1)}, s32[8,256]{1,0:T(8,128)S(1)}, u32[]{:S(2)}, u32[]{:S(2)}) collective-permute-start(s32[8,256]{1,0:T(8,128)S(1)} %shard_map.94.refs_0_), channel_id=1, source_target_pairs={{0,160},{32,192},{64,224},{96,0},{128,32},{160,64},{192,96},{224,1... | collective-permute-start | bytes 24584 | tf_op jit(solution)/shard_map/ppermute | solution.py:213
  89.4 12.1 %collective-permute-start.20 = (bf16[304,640]{1,0:T(8,128)(2,1)S(1)}, bf16[304,640]{1,0:T(8,128)(2,1)S(1)}, u32[]{:S(2)}, u32[]{:S(2)}) collective-permute-start(bf16[304,640]{1,0:T(8,128)(2,1)S(1)} %get-tuple-element.23.refs_0_), channel_id=1, source_target_pairs={{0,32},{32,64},{64,96},{96,128},{128,160},{160,192},{192,224},{224... | collective-permute-start | bytes 1167368 | tf_op jit(solution)/shard_map/ppermute | solution.py:213
  91.0 10.5 %collective-permute-start.24 = (bf16[304,640]{1,0:T(8,128)(2,1)S(1)}, bf16[304,640]{1,0:T(8,128)(2,1)S(1)}, u32[]{:S(2)}, u32[]{:S(2)}) collective-permute-start(bf16[304,640]{1,0:T(8,128)(2,1)S(1)} %get-tuple-element.23.refs_0_), channel_id=1, source_target_pairs={{0,224},{32,0},{64,32},{96,64},{128,96},{160,128},{192,160},{224,1... | collective-permute-start | bytes 1167368 | tf_op jit(solution)/shard_map/ppermute | solution.py:213
  101.5 18.7 %collective-permute-start.21 = (bf16[304,640]{1,0:T(8,128)(2,1)S(1)}, bf16[304,640]{1,0:T(8,128)(2,1)S(1)}, u32[]{:S(2)}, u32[]{:S(2)}) collective-permute-start(bf16[304,640]{1,0:T(8,128)(2,1)S(1)} %collective-permute-done.20.refs_1_), channel_id=1, source_target_pairs={{0,32},{32,64},{64,96},{96,128},{128,160},{160,192},{192,224},{224... | collective-permute-start | bytes 1167368 | tf_op jit(solution)/shard_map/ppermute | solution.py:213
  101.5 18.7 %collective-permute-start.25 = (bf16[304,640]{1,0:T(8,128)(2,1)S(1)}, bf16[304,640]{1,0:T(8,128)(2,1)S(1)}, u32[]{:S(2)}, u32[]{:S(2)}) collective-permute-start(bf16[304,640]{1,0:T(8,128)(2,1)S(1)} %collective-permute-done.24.refs_2_), channel_id=1, source_target_pairs={{0,224},{32,0},{64,32},{96,64},{128,96},{160,128},{192,160},{224,1... | collective-permute-start | bytes 1167368 | tf_op jit(solution)/shard_map/ppermute | solution.py:213
  108.6 8.4 %collective-permute-start.12 = (bf16[208,640]{1,0:T(8,128)(2,1)S(1)}, bf16[208,640]{1,0:T(8,128)(2,1)S(1)}, u32[]{:S(2)}, u32[]{:S(2)}) collective-permute-start(bf16[208,640]{1,0:T(8,128)(2,1)S(1)} %get-tuple-element.22.refs_5_), channel_id=1, source_target_pairs={{0,32},{32,64},{64,96},{96,128},{128,160},{160,192},{192,224},{224... | collective-permute-start | bytes 798728 | tf_op jit(solution)/shard_map/ppermute | solution.py:213
  108.7 8.3 %collective-permute-start.16 = (bf16[208,640]{1,0:T(8,128)(2,1)S(1)}, bf16[208,640]{1,0:T(8,128)(2,1)S(1)}, u32[]{:S(2)}, u32[]{:S(2)}) collective-permute-start(bf16[208,640]{1,0:T(8,128)(2,1)S(1)} %get-tuple-element.22.refs_5_), channel_id=1, source_target_pairs={{0,224},{32,0},{64,32},{96,64},{128,96},{160,128},{192,160},{224,1... | collective-permute-start | bytes 798728 | tf_op jit(solution)/shard_map/ppermute | solution.py:213
  117.0 10.5 %collective-permute-start.13 = (bf16[208,640]{1,0:T(8,128)(2,1)S(1)}, bf16[208,640]{1,0:T(8,128)(2,1)S(1)}, u32[]{:S(2)}, u32[]{:S(2)}) collective-permute-start(bf16[208,640]{1,0:T(8,128)(2,1)S(1)} %collective-permute-done.12.refs_6_), channel_id=1, source_target_pairs={{0,32},{32,64},{64,96},{96,128},{128,160},{160,192},{192,224},{224... | collective-permute-start | bytes 798728 | tf_op jit(solution)/shard_map/ppermute | solution.py:213
  117.0 10.5 %collective-permute-start.17 = (bf16[208,640]{1,0:T(8,128)(2,1)S(1)}, bf16[208,640]{1,0:T(8,128)(2,1)S(1)}, u32[]{:S(2)}, u32[]{:S(2)}) collective-permute-start(bf16[208,640]{1,0:T(8,128)(2,1)S(1)} %collective-permute-done.16.refs_7_), channel_id=1, source_target_pairs={{0,224},{32,0},{64,32},{96,64},{128,96},{160,128},{192,160},{224,1... | collective-permute-start | bytes 798728 | tf_op jit(solution)/shard_map/ppermute | solution.py:213
  120.2 15.6 %collective-permute-start.22 = (bf16[304,640]{1,0:T(8,128)(2,1)S(1)}, bf16[304,640]{1,0:T(8,128)(2,1)S(1)}, u32[]{:S(2)}, u32[]{:S(2)}) collective-permute-start(bf16[304,640]{1,0:T(8,128)(2,1)S(1)} %collective-permute-done.21.refs_3_), channel_id=1, source_target_pairs={{0,32},{32,64},{64,96},{96,128},{128,160},{160,192},{192,224},{224... | collective-permute-start | bytes 1167368 | tf_op jit(solution)/shard_map/ppermute | solution.py:213
  120.3 15.7 %collective-permute-start.26 = (bf16[304,640]{1,0:T(8,128)(2,1)S(1)}, bf16[304,640]{1,0:T(8,128)(2,1)S(1)}, u32[]{:S(2)}, u32[]{:S(2)}) collective-permute-start(bf16[304,640]{1,0:T(8,128)(2,1)S(1)} %collective-permute-done.25.refs_4_), channel_id=1, source_target_pairs={{0,224},{32,0},{64,32},{96,64},{128,96},{160,128},{192,160},{224,1... | collective-permute-start | bytes 1167368 | tf_op jit(solution)/shard_map/ppermute | solution.py:213
  127.5 14.0 %collective-permute-start.14 = (bf16[208,640]{1,0:T(8,128)(2,1)S(1)}, bf16[208,640]{1,0:T(8,128)(2,1)S(1)}, u32[]{:S(2)}, u32[]{:S(2)}) collective-permute-start(bf16[208,640]{1,0:T(8,128)(2,1)S(1)} %collective-permute-done.13.refs_8_), channel_id=1, source_target_pairs={{0,32},{32,64},{64,96},{96,128},{128,160},{160,192},{192,224},{224... | collective-permute-start | bytes 798728 | tf_op jit(solution)/shard_map/ppermute | solution.py:213
  127.5 14.1 %collective-permute-start.18 = (bf16[208,640]{1,0:T(8,128)(2,1)S(1)}, bf16[208,640]{1,0:T(8,128)(2,1)S(1)}, u32[]{:S(2)}, u32[]{:S(2)}) collective-permute-start(bf16[208,640]{1,0:T(8,128)(2,1)S(1)} %collective-permute-done.17.refs_9_), channel_id=1, source_target_pairs={{0,224},{32,0},{64,32},{96,64},{128,96},{160,128},{192,160},{224,1... | collective-permute-start | bytes 798728 | tf_op jit(solution)/shard_map/ppermute | solution.py:213
  135.8 12.0 %collective-permute-start.23 = (bf16[152,640]{1,0:T(8,128)(2,1)S(1)}, bf16[152,640]{1,0:T(8,128)(2,1)S(1)}, u32[]{:S(2)}, u32[]{:S(2)}) collective-permute-start(bf16[152,640]{1,0:T(8,128)(2,1)S(1)} %slice.18), channel_id=1, source_target_pairs={{0,32},{32,64},{64,96},{96,128},{128,160},{160,192},{192,224},{224... | collective-permute-start | bytes 583688 | tf_op jit(solution)/shard_map/ppermute | solution.py:213
  136.0 11.9 %collective-permute-start.27 = (bf16[152,640]{1,0:T(8,128)(2,1)S(1)}, bf16[152,640]{1,0:T(8,128)(2,1)S(1)}, u32[]{:S(2)}, u32[]{:S(2)}) collective-permute-start(bf16[152,640]{1,0:T(8,128)(2,1)S(1)} %slice.19), channel_id=1, source_target_pairs={{0,224},{32,0},{64,32},{96,64},{128,96},{160,128},{192,160},{224,1... | collective-permute-start | bytes 583688 | tf_op jit(solution)/shard_map/ppermute | solution.py:213
  141.5 7.1 %collective-permute-start.15 = (bf16[104,640]{1,0:T(8,128)(2,1)S(1)}, bf16[104,640]{1,0:T(8,128)(2,1)S(1)}, u32[]{:S(2)}, u32[]{:S(2)}) collective-permute-start(bf16[104,640]{1,0:T(8,128)(2,1)S(1)} %slice.16), channel_id=1, source_target_pairs={{0,32},{32,64},{64,96},{96,128},{128,160},{160,192},{192,224},{224... | collective-permute-start | bytes 399368 | tf_op jit(solution)/shard_map/ppermute | solution.py:213
  141.7 7.0 %collective-permute-start.19 = (bf16[104,640]{1,0:T(8,128)(2,1)S(1)}, bf16[104,640]{1,0:T(8,128)(2,1)S(1)}, u32[]{:S(2)}, u32[]{:S(2)}) collective-permute-start(bf16[104,640]{1,0:T(8,128)(2,1)S(1)} %slice.17), channel_id=1, source_target_pairs={{0,224},{32,0},{64,32},{96,64},{128,96},{160,128},{192,160},{224,1... | collective-permute-start | bytes 399368 | tf_op jit(solution)/shard_map/ppermute | solution.py:213
